TPU v7x, 32 devices: a whole 2x2x4 slice. The times are simulated.
32 devices in a mesh: shard: 4 (over x, core), replica: 8 (over z, y).
Axes of the slice: x: 2, y: 2, z: 4, core: 2. Of those that a mesh axis runs over, the one named last changes fastest.
Arguments:
- tokens: bfloat16 [16384, 768], P(('shard', 'replica')), may hold values from -6 to 6
- cotangent: bfloat16 [16384, 768], P(('shard', 'replica')), may hold values from -6 to 6
- lengths: int32 [32], replicated, may hold values from 16 to 512, as said below
- assignment: int32 [32], replicated, may hold values from 0 to 31, as said below
- positions: int32 [16384], P(('shard', 'replica')), may hold values from 0 to 2047, as said below
- attention_gain: bfloat16 [768], P('shard'), may hold values from 0.25 to 2.5
- query_weight: bfloat16 [768, 768], P('shard'), may hold values from -0.21875 to 0.21875
- key_weight: bfloat16 [768, 768], P('shard'), may hold values from -0.21875 to 0.21875
- value_weight: bfloat16 [768, 768], P('shard'), may hold values from -0.21875 to 0.21875
- out_weight: bfloat16 [768, 768], P('shard'), may hold values from -1.25 to 1.25
- feedforward_gain: bfloat16 [768], P('shard'), may hold values from 0.25 to 2.5
- gate_weight: bfloat16 [768, 3072], P('shard'), may hold values from -0.21875 to 0.21875
- up_weight: bfloat16 [768, 3072], P('shard'), may hold values from -0.21875 to 0.21875
- down_weight: bfloat16 [3072, 768], P('shard'), may hold values from -0.21875 to 0.21875
Outputs:
- output: bfloat16 [16384, 768], P(('shard', 'replica'))
- input_grad: float32 [16384, 768], P(('shard', 'replica'))
- attention_gain_grad: float32 [768], P('shard')
- query_grad: float32 [768, 768], P('shard')
- key_grad: float32 [768, 768], P('shard')
- value_grad: float32 [768, 768], P('shard')
- out_grad: float32 [768, 768], P('shard')
- feedforward_gain_grad: float32 [768], P('shard')
- gate_grad: float32 [768, 3072], P('shard')
- up_grad: float32 [768, 3072], P('shard')
- down_grad: float32 [3072, 768], P('shard')
Inputs may be any that keep to these rules, and one draw needn't show every extreme that they name: `lengths`: each block holds exactly 1 sequence, 16 to 512 rows long; in some block it is exactly 512 rows long. `assignment`: every block index is named by exactly 1 sequence. Within a sequence, positions rise by one from row to row from a start between 0 and 2048 minus the sequence's length; empty rows hold 0.
All inputs are finite; a program needn't handle non-finite values.
Results may differ from a plain program's by a relative error of at most 0.023.
Values may be sent and summed in bfloat16 or wider, within the bound.
A program may use at most 192 MiB of HBM per device.

v0:
```python
import math

import jax
import jax.numpy as jnp
from jax import lax
from jax.sharding import PartitionSpec as P

HEADS = 12
HDIM = 64


EPSILON = 1e-05
ROPE_BASE = 10000.0


def rms_scale(values):
    return lax.rsqrt(jnp.mean(values * values, axis=-1, keepdims=True) + EPSILON)


def rotation(positions, head_size):
    half_size = head_size // 2
    steps_range = jnp.arange(half_size, dtype=jnp.float32)
    frequency = jnp.exp(steps_range * (-2.0 * math.log(ROPE_BASE) / head_size))
    angles = positions.astype(jnp.float32)[:, None] * frequency[None, :]
    return (jnp.cos(angles), jnp.sin(angles))


def rotate(values, cosine_table, sine_table):
    half_size = cosine_table.shape[1]
    shaped = values.reshape(values.shape[0], -1, 2 * half_size)
    first_half = shaped[..., :half_size]
    second_half = shaped[..., half_size:]
    cos_rows = cosine_table[:, None, :]
    sin_rows = sine_table[:, None, :]
    turned = jnp.concatenate(
        [
            first_half * cos_rows - second_half * sin_rows,
            second_half * cos_rows + first_half * sin_rows,
        ],
        axis=-1,
    )
    return turned.reshape(values.shape)


def rotate_back(values, cosine_table, sine_table):
    half_size = cosine_table.shape[1]
    shaped = values.reshape(values.shape[0], -1, 2 * half_size)
    first_half = shaped[..., :half_size]
    second_half = shaped[..., half_size:]
    cos_rows = cosine_table[:, None, :]
    sin_rows = sine_table[:, None, :]
    turned = jnp.concatenate(
        [
            first_half * cos_rows + second_half * sin_rows,
            second_half * cos_rows - first_half * sin_rows,
        ],
        axis=-1,
    )
    return turned.reshape(values.shape)


def sequence_mask(lengths, assignment, device, slot_count):
    owned_lengths = jnp.where(assignment == device, lengths, 0)
    seq_ends = jnp.cumsum(owned_lengths)
    slot_ids = jnp.arange(slot_count, dtype=jnp.int32)
    labels = jnp.sum((seq_ends[None, :] <= slot_ids[:, None]).astype(jnp.int32), axis=1)
    allowed = (labels[:, None] == labels[None, :]) & (slot_ids[None, :] <= slot_ids[:, None])
    valid_rows = (slot_ids < seq_ends[-1]).astype(jnp.float32)[:, None]
    return (allowed, valid_rows)


def by_group(values, groups):
    return jnp.moveaxis(values.reshape(values.shape[0], groups, -1, HDIM), 1, 0)


def from_group(values):
    moved = jnp.moveaxis(values, 0, 1)
    return moved.reshape(moved.shape[0], -1)


def norm_back(grad_normed, values, scale_rows, gain):
    scaled_grad = gain * grad_normed
    gain_grad = jnp.sum(grad_normed * values * scale_rows, axis=0)
    grad_values = scale_rows * scaled_grad - values * scale_rows**3 * jnp.mean(
        scaled_grad * values, axis=-1, keepdims=True
    )
    return (gain_grad, grad_values)


def per_device(
    tokens,
    cotangent,
    lengths,
    assignment,
    positions,
    attention_gain,
    query_weight,
    key_weight,
    value_weight,
    out_weight,
    feedforward_gain,
    gate_weight,
    up_weight,
    down_weight,
):
    slot_count = tokens.shape[0]
    heads_per = math.gcd(HEADS, 4)
    groups = HEADS // heads_per
    inv_root = 1.0 / math.sqrt(HDIM)
    device = lax.axis_index("shard") * lax.axis_size("replica") + lax.axis_index("replica")
    allowed, valid_rows = sequence_mask(lengths, assignment, device, slot_count)
    cosine_table, sine_table = rotation(positions, HDIM)
    gain_one, w_query, w_key, w_value, w_out = (
        lax.all_gather(attention_gain, "shard", axis=0, tiled=True),
        lax.all_gather(query_weight, "shard", axis=0, tiled=True),
        lax.all_gather(key_weight, "shard", axis=0, tiled=True),
        lax.all_gather(value_weight, "shard", axis=0, tiled=True),
        lax.all_gather(out_weight, "shard", axis=0, tiled=True),
    )
    values = tokens.astype(jnp.float32)
    scale_one = rms_scale(values)
    normed = (values * scale_one * gain_one.astype(jnp.float32)).astype(jnp.bfloat16)
    query_lin = jnp.dot(normed, w_query, preferred_element_type=jnp.float32)
    key_lin = jnp.dot(normed, w_key, preferred_element_type=jnp.float32)
    value_low = jnp.dot(normed, w_value, preferred_element_type=jnp.float32).astype(jnp.bfloat16)
    query_rot = rotate(query_lin, cosine_table, sine_table).astype(jnp.bfloat16)
    key_rot = rotate(key_lin, cosine_table, sine_table).astype(jnp.bfloat16)
    query_groups = by_group(query_rot, groups)
    key_groups = by_group(key_rot, groups)
    value_groups = by_group(value_low, groups)

    def attend(group_in):
        query_part, key_part, value_part = group_in
        scores = (
            jnp.einsum("qhd,khd->hqk", query_part, key_part, preferred_element_type=jnp.float32)
            * inv_root
        )
        scores = jnp.where(allowed[None], scores, -jnp.inf)
        row_peak = jnp.max(scores, axis=-1, keepdims=True)
        exponent = jnp.exp(scores - row_peak)
        row_total = jnp.sum(exponent, axis=-1, keepdims=True)
        probability = (exponent / row_total).astype(jnp.bfloat16)
        mixed_values = jnp.einsum(
            "hqk,khd->qhd", probability, value_part, preferred_element_type=jnp.float32
        )
        return (mixed_values, row_peak[..., 0] + jnp.log(row_total[..., 0]))

    mixed_groups, log_totals = lax.map(attend, (query_groups, key_groups, value_groups))
    attended = from_group(mixed_groups).astype(jnp.bfloat16)
    hidden_one = values + jnp.dot(attended, w_out, preferred_element_type=jnp.float32)
    gain_two, w_gate, w_up, w_down = (
        lax.all_gather(feedforward_gain, "shard", axis=0, tiled=True),
        lax.all_gather(gate_weight, "shard", axis=0, tiled=True),
        lax.all_gather(up_weight, "shard", axis=0, tiled=True),
        lax.all_gather(down_weight, "shard", axis=0, tiled=True),
    )
    scale_two = rms_scale(hidden_one)
    normed_two = (hidden_one * scale_two * gain_two.astype(jnp.float32)).astype(jnp.bfloat16)
    gate = jnp.dot(normed_two, w_gate, preferred_element_type=jnp.float32)
    upward = jnp.dot(normed_two, w_up, preferred_element_type=jnp.float32)
    sigmoid_gate = jax.nn.sigmoid(gate)
    activated = gate * sigmoid_gate
    hidden = (activated * upward).astype(jnp.bfloat16)
    branch_two = jnp.dot(hidden, w_down, preferred_element_type=jnp.float32)
    output = ((hidden_one + branch_two) * valid_rows).astype(jnp.bfloat16)
    gain_two, w_gate, w_up, w_down = (
        lax.all_gather(feedforward_gain, "shard", axis=0, tiled=True),
        lax.all_gather(gate_weight, "shard", axis=0, tiled=True),
        lax.all_gather(up_weight, "shard", axis=0, tiled=True),
        lax.all_gather(down_weight, "shard", axis=0, tiled=True),
    )
    grad_out = cotangent.astype(jnp.float32) * valid_rows
    grad_branch_two = grad_out.astype(jnp.bfloat16)
    grad_down = jnp.einsum("nf,nd->fd", hidden, grad_branch_two, preferred_element_type=jnp.float32)
    grad_hidden = jnp.einsum(
        "nd,fd->nf", grad_branch_two, w_down, preferred_element_type=jnp.float32
    )
    grad_gate = (grad_hidden * upward * sigmoid_gate * (1.0 + gate * (1.0 - sigmoid_gate))).astype(
        jnp.bfloat16
    )
    grad_up = (grad_hidden * activated).astype(jnp.bfloat16)
    grad_gate_weight = jnp.einsum(
        "nd,nf->df", normed_two, grad_gate, preferred_element_type=jnp.float32
    )
    grad_up_weight = jnp.einsum(
        "nd,nf->df", normed_two, grad_up, preferred_element_type=jnp.float32
    )
    grad_normed_two = jnp.einsum(
        "nf,df->nd", grad_gate, w_gate, preferred_element_type=jnp.float32
    ) + jnp.einsum("nf,df->nd", grad_up, w_up, preferred_element_type=jnp.float32)
    grad_gain_two, grad_norm_two = norm_back(
        grad_normed_two, hidden_one, scale_two, gain_two.astype(jnp.float32)
    )
    grad_hidden_one = grad_out + grad_norm_two
    ffn_terms = (grad_gain_two, grad_gate_weight, grad_up_weight, grad_down)
    ffn_shares = (
        lax.psum_scatter(
            ffn_terms[0].astype(jnp.bfloat16), "shard", scatter_dimension=0, tiled=True
        ).astype(jnp.float32),
        lax.psum_scatter(
            ffn_terms[1].astype(jnp.bfloat16), "shard", scatter_dimension=0, tiled=True
        ).astype(jnp.float32),
        lax.psum_scatter(
            ffn_terms[2].astype(jnp.bfloat16), "shard", scatter_dimension=0, tiled=True
        ).astype(jnp.float32),
        lax.psum_scatter(
            ffn_terms[3].astype(jnp.bfloat16), "shard", scatter_dimension=0, tiled=True
        ).astype(jnp.float32),
    )
    ffn_sums = (
        lax.psum(ffn_shares[0].astype(jnp.bfloat16), "replica").astype(jnp.float32),
        lax.psum(ffn_shares[1].astype(jnp.bfloat16), "replica").astype(jnp.float32),
        lax.psum(ffn_shares[2].astype(jnp.bfloat16), "replica").astype(jnp.float32),
        lax.psum(ffn_shares[3].astype(jnp.bfloat16), "replica").astype(jnp.float32),
    )
    gain_one, w_query, w_key, w_value, w_out = (
        lax.all_gather(attention_gain, "shard", axis=0, tiled=True),
        lax.all_gather(query_weight, "shard", axis=0, tiled=True),
        lax.all_gather(key_weight, "shard", axis=0, tiled=True),
        lax.all_gather(value_weight, "shard", axis=0, tiled=True),
        lax.all_gather(out_weight, "shard", axis=0, tiled=True),
    )
    grad_branch_one = grad_hidden_one.astype(jnp.bfloat16)
    grad_out_weight = jnp.einsum(
        "nd,ne->de", attended, grad_branch_one, preferred_element_type=jnp.float32
    )
    grad_attended = jnp.einsum(
        "ne,de->nd", grad_branch_one, w_out, preferred_element_type=jnp.float32
    ).astype(jnp.bfloat16)
    grad_groups = by_group(grad_attended, groups)

    def attend_back(group_in):
        query_part, key_part, value_part, grad_part, log_total = group_in
        scores = (
            jnp.einsum("qhd,khd->hqk", query_part, key_part, preferred_element_type=jnp.float32)
            * inv_root
        )
        scores = jnp.where(allowed[None], scores, -jnp.inf)
        probability = jnp.exp(scores - log_total[..., None])
        probability_low = probability.astype(jnp.bfloat16)
        grad_value = jnp.einsum(
            "hqk,qhd->khd", probability_low, grad_part, preferred_element_type=jnp.float32
        )
        grad_probability = jnp.einsum(
            "qhd,khd->hqk", grad_part, value_part, preferred_element_type=jnp.float32
        )
        row_dot = jnp.sum(probability * grad_probability, axis=-1, keepdims=True)
        grad_scores = (probability * (grad_probability - row_dot)).astype(jnp.bfloat16)
        grad_query = (
            jnp.einsum("hqk,khd->qhd", grad_scores, key_part, preferred_element_type=jnp.float32)
            * inv_root
        )
        grad_key = (
            jnp.einsum("hqk,qhd->khd", grad_scores, query_part, preferred_element_type=jnp.float32)
            * inv_root
        )
        return (grad_query, grad_key, grad_value)

    grad_query_groups, grad_key_groups, grad_value_groups = lax.map(
        attend_back, (query_groups, key_groups, value_groups, grad_groups, log_totals)
    )
    grad_query_lin = rotate_back(from_group(grad_query_groups), cosine_table, sine_table).astype(
        jnp.bfloat16
    )
    grad_key_lin = rotate_back(from_group(grad_key_groups), cosine_table, sine_table).astype(
        jnp.bfloat16
    )
    grad_value_lin = from_group(grad_value_groups).astype(jnp.bfloat16)
    grad_query_weight = jnp.einsum(
        "nd,ne->de", normed, grad_query_lin, preferred_element_type=jnp.float32
    )
    grad_key_weight = jnp.einsum(
        "nd,ne->de", normed, grad_key_lin, preferred_element_type=jnp.float32
    )
    grad_value_weight = jnp.einsum(
        "nd,ne->de", normed, grad_value_lin, preferred_element_type=jnp.float32
    )
    grad_normed = jnp.einsum(
        "ne,de->nd", grad_query_lin, w_query, preferred_element_type=jnp.float32
    )
    grad_normed = grad_normed + jnp.einsum(
        "ne,de->nd", grad_key_lin, w_key, preferred_element_type=jnp.float32
    )
    grad_normed = grad_normed + jnp.einsum(
        "ne,de->nd", grad_value_lin, w_value, preferred_element_type=jnp.float32
    )
    grad_gain_one, grad_norm_one = norm_back(
        grad_normed, values, scale_one, gain_one.astype(jnp.float32)
    )
    input_grad = grad_hidden_one + grad_norm_one
    attn_terms = (
        grad_gain_one,
        grad_query_weight,
        grad_key_weight,
        grad_value_weight,
        grad_out_weight,
    )
    attn_shares = (
        lax.psum_scatter(
            attn_terms[0].astype(jnp.bfloat16), "shard", scatter_dimension=0, tiled=True
        ).astype(jnp.float32),
        lax.psum_scatter(
            attn_terms[1].astype(jnp.bfloat16), "shard", scatter_dimension=0, tiled=True
        ).astype(jnp.float32),
        lax.psum_scatter(
            attn_terms[2].astype(jnp.bfloat16), "shard", scatter_dimension=0, tiled=True
        ).astype(jnp.float32),
        lax.psum_scatter(
            attn_terms[3].astype(jnp.bfloat16), "shard", scatter_dimension=0, tiled=True
        ).astype(jnp.float32),
        lax.psum_scatter(
            attn_terms[4].astype(jnp.bfloat16), "shard", scatter_dimension=0, tiled=True
        ).astype(jnp.float32),
    )
    attn_sums = (
        lax.psum(attn_shares[0].astype(jnp.bfloat16), "replica").astype(jnp.float32),
        lax.psum(attn_shares[1].astype(jnp.bfloat16), "replica").astype(jnp.float32),
        lax.psum(attn_shares[2].astype(jnp.bfloat16), "replica").astype(jnp.float32),
        lax.psum(attn_shares[3].astype(jnp.bfloat16), "replica").astype(jnp.float32),
        lax.psum(attn_shares[4].astype(jnp.bfloat16), "replica").astype(jnp.float32),
    )
    return (
        output,
        input_grad,
        attn_sums[0],
        attn_sums[1],
        attn_sums[2],
        attn_sums[3],
        attn_sums[4],
        ffn_sums[0],
        ffn_sums[1],
        ffn_sums[2],
        ffn_sums[3],
    )


def solution(mesh):
    return jax.shard_map(
        per_device,
        mesh=mesh,
        in_specs=(
            P(("shard", "replica"), None),
            P(("shard", "replica"), None),
            P(),
            P(),
            P(("shard", "replica")),
            P("shard"),
            P("shard", None),
            P("shard", None),
            P("shard", None),
            P("shard", None),
            P("shard"),
            P("shard", None),
            P("shard", None),
            P("shard", None),
        ),
        out_specs=(
            P(("shard", "replica"), None),
            P(("shard", "replica"), None),
            P("shard"),
            P("shard", None),
            P("shard", None),
            P("shard", None),
            P("shard", None),
            P("shard"),
            P("shard", None),
            P("shard", None),
            P("shard", None),
        ),
        check_vma=False,
    )
```

profile of v0, /device:TPU:0, one launch (start us, length us, event | category | flops | bytes accessed | tf_op | source)
XLA Modules:
  0.0 718.2 jit_solution(7855634631792464619)
XLA Ops:
  15.5 8.7 %all-reduce.7 = (bf16[768]{0:T(1024)(128)(2,1)S(1)}, bf16[768]{0:T(1024)(128)(2,1)S(1)}) all-reduce(bf16[768]{0:T(1024)(128)(2,1)S(1)} %dynamic-update-slice, bf16[768]{0:T(1024)(128)(2,1)S(1)} %dynamic-update-slice.1), channel_id=1, replica_groups=mesh['shard'=4,'replica'=8] {'shard'}, use_global_device_ids=true, to_apply=%add | all-reduce | flops 1536 | bytes 6144
  33.1 15.8 %all-gather.10.cloned.1.call-done = bf16[768,768]{1,0:T(8,128)(2,1)} async-done(((bf16[192,768]{1,0:T(8,128)(2,1)}), bf16[768,768]{1,0:T(8,128)(2,1)}) %all-gather.10.cloned.1.call-update) | async-done | bytes 1179664 | tf_op jit(solution)/shard_map/all_gather | solution.py:115
  51.1 16.9 %all-gather.12.cloned.1.call-done = bf16[768,768]{1,0:T(8,128)(2,1)} async-done(((bf16[192,768]{1,0:T(8,128)(2,1)}), bf16[768,768]{1,0:T(8,128)(2,1)}) %all-gather.12.cloned.1.call-update) | async-done | bytes 1179664 | tf_op jit(solution)/shard_map/all_gather | solution.py:116
  70.8 15.3 %while.30 = (s32[]{:T(128)}, bf16[3,512,4,64]{1,3,2,0:T(8,128)(2,1)}, f32[3,4,512]{2,1,0:T(4,128)S(1)}, bf16[3,512,4,64]{1,3,2,0:T(8,128)(2,1)}, bf16[3,512,4,64...) while((s32[]{:T(128)}, ...), condition=%wide.region_6.7_spmd.clone.clone, body=%wide.region_3.6_spmd.clone.sunk.clone | while | flops 281802752 | bytes 15011921 | solution.py:148
  90.6 35.1 %all-gather.16.cloned.1.call-done = bf16[768,3072]{1,0:T(8,128)(2,1)} async-done(((bf16[192,3072]{1,0:T(8,128)(2,1)}), bf16[768,3072]{1,0:T(8,128)(2,1)}) %all-gather.16.cloned.1.call-update) | async-done | bytes 4718608 | tf_op jit(solution)/shard_map/all_gather | solution.py:153
  125.7 6.8 fusion.87
  132.5 32.1 %all-gather.18.cloned.1.call-done = bf16[768,3072]{1,0:T(8,128)(2,1)} async-done(((bf16[192,3072]{1,0:T(8,128)(2,1)}), bf16[768,3072]{1,0:T(8,128)(2,1)}) %all-gather.18.cloned.1.call-update) | async-done | bytes 4718608 | tf_op jit(solution)/shard_map/all_gather | solution.py:154
  164.6 6.8 fusion.88
  171.4 32.2 %all-gather.20.cloned.1.call-done = bf16[3072,768]{1,0:T(8,128)(2,1)} async-done(((bf16[768,768]{1,0:T(8,128)(2,1)}), bf16[3072,768]{1,0:T(8,128)(2,1)}) %all-gather.20.cloned.1.call-update) | async-done | bytes 4718608 | tf_op jit(solution)/shard_map/all_gather | solution.py:155
  203.6 10.1 %multiply_convert_fusion.1 = (bf16[512,3072]{1,0:T(8,128)(2,1)S(1)}, bf16[512,3072]{1,0:T(8,128)(2,1)S(1)}, bf16[512,3072]{1,0:T(8,128)(2,1)}) fusion(f32[512,3072]{1,0:T(8,128)} %fusion.87, f32[512,3072]{1,0:T(8,128)} %fusion.88, bf16[3072,768]{1,0:T(8,128)(2,1)} %all-gather.20.cloned.1.call-done, bf16[512,768]{1,0:T(8,128)(2,1)S(1)} %copy-done.12, ...), kind=kOutput, calls=%fused_computation.64 | convolution fusion | flops 2440691712 | bytes 27527168 | tf_op jit(solution)/shard_map/nd,fd->nf/dot_general | solution.py:175
  213.7 7.3 %fusion.89 = f32[512,768]{1,0:T(8,128)S(1)} fusion(bf16[512,3072]{1,0:T(8,128)(2,1)S(1)} %get-tuple-element.204, bf16[768,3072]{1,0:T(8,128)(2,1)} %all-gather.16.cloned.1.call-done), kind=kOutput, calls=%fused_computation.139 | convolution fusion | flops 2415919104 | bytes 9437184 | tf_op jit(solution)/shard_map/nf,df->nd/dot_general | solution.py:188
  229.4 29.0 %while.31 = (s32[]{:T(128)}, f32[3,512,4,64]{1,3,2,0:T(8,128)}, f32[3,512,4,64]{1,3,2,0:T(8,128)}, bf16[3,512,4,64]{1,3,2,0:T(8,128)(2,1)}, bf16[3,512,4,64]{1,3...) while((s32[]{:T(128)}, f32[3,512,4,64]{1,3,2,0:T(8,128)}, ...), condition=%wide.region_11.12_spmd.clone.clone, body=%wide.region_9.11_spmd.clone.sunk.clone | while | flops 687863808 | bytes 39124100 | solution.py:259
  273.6 6.2 convolution_convert_fusion.2
  279.9 6.3 convolution_convert_fusion.1
  287.4 6.8 convolution_convert_fusion
  294.3 24.4 %reduce-scatter.8.cloned.1.call-done = bf16[192,768]{1,0:T(8,128)(2,1)} async-done(((bf16[768,768]{1,0:T(8,128)(2,1)}), bf16[192,768]{1,0:T(8,128)(2,1)}) %reduce-scatter.8.cloned.1.call-update) | async-done | bytes 294928 | tf_op jit(solution)/shard_map/reduce_scatter | solution.py:302
  318.7 28.1 %reduce-scatter.14.cloned.1.call-done = bf16[192,768]{1,0:T(8,128)(2,1)} async-done(((bf16[768,768]{1,0:T(8,128)(2,1)}), bf16[192,768]{1,0:T(8,128)(2,1)}) %reduce-scatter.14.cloned.1.call-update) | async-done | bytes 294928 | tf_op jit(solution)/shard_map/reduce_scatter | solution.py:311
  346.8 28.8 %reduce-scatter.12.cloned.1.call-done = bf16[192,768]{1,0:T(8,128)(2,1)} async-done(((bf16[768,768]{1,0:T(8,128)(2,1)}), bf16[192,768]{1,0:T(8,128)(2,1)}) %reduce-scatter.12.cloned.1.call-update) | async-done | bytes 294928 | tf_op jit(solution)/shard_map/reduce_scatter | solution.py:308
  375.6 50.4 %reduce-scatter.16.cloned.1.call-done = bf16[192,3072]{1,0:T(8,128)(2,1)} async-done(((bf16[768,3072]{1,0:T(8,128)(2,1)}), bf16[192,3072]{1,0:T(8,128)(2,1)}) %reduce-scatter.16.cloned.1.call-update) | async-done | bytes 1179664 | tf_op jit(solution)/shard_map/reduce_scatter | solution.py:200
  426.0 50.5 %reduce-scatter.18.cloned.1.call-done = bf16[192,3072]{1,0:T(8,128)(2,1)} async-done(((bf16[768,3072]{1,0:T(8,128)(2,1)}), bf16[192,3072]{1,0:T(8,128)(2,1)}) %reduce-scatter.18.cloned.1.call-update) | async-done | bytes 1179664 | tf_op jit(solution)/shard_map/reduce_scatter | solution.py:203
  476.5 50.4 %reduce-scatter.20.cloned.1.call-done = bf16[768,768]{1,0:T(8,128)(2,1)} async-done(((bf16[3072,768]{1,0:T(8,128)(2,1)}), bf16[768,768]{1,0:T(8,128)(2,1)}) %reduce-scatter.20.cloned.1.call-update) | async-done | bytes 1179664 | tf_op jit(solution)/shard_map/reduce_scatter | solution.py:206
  540.9 23.0 %all-reduce.4 = (bf16[192]{0:T(256)(128)(2,1)S(1)}, bf16[192]{0:T(256)(128)(2,1)S(1)}) all-reduce(bf16[192]{0:T(256)(128)(2,1)S(1)} %dynamic-slice.3, bf16[192]{0:T(256)(128)(2,1)S(1)} %dynamic-slice.5), channel_id=1, replica_groups=mesh['shard'=4,'replica'=8] {'replica'}, use_global_device_ids=true, to_apply=%region_15.16 | all-reduce | flops 384 | bytes 1536 | tf_op jit(solution)/shard_map/psum | solution.py:316
  568.2 5.9 multiply_convert_fusion.4
  574.1 127.4 %all-reduce.10.cloned.1.call-done = (bf16[192,768]{1,0:T(8,128)(2,1)}, bf16[192,768]{1,0:T(8,128)(2,1)}, bf16[192,768]{1,0:T(8,128)(2,1)}, bf16[192,768]{1,0:T(8...) async-done(((bf16[192,768]{1,0:T(8,128)(2,1)}, bf16[192,768]{1,0:T(8,128)(2,1)}, bf16[192,768]{1,0:T(8,128)(2,1)}, ...) | async-done | bytes 4718608 | tf_op jit(solution)/shard_map/psum | solution.py:317
  (208 shorter events, 121.7 us)
Async XLA Ops:
  7.2 22.6 %all-gather.8.cloned.1.call-start = ((), (), s32[]{:S(2)}) async-start(), calls=%async_computation.7 | async-start | bytes 1474560 | tf_op jit(solution)/shard_map/all_gather | solution.py:117
  7.9 41.0 %all-gather.10.cloned.1.call-start = ((), (), s32[]{:S(2)}) async-start(), calls=%async_computation.8 | async-start | bytes 1474560 | tf_op jit(solution)/shard_map/all_gather | solution.py:115
  8.7 59.3 %all-gather.12.cloned.1.call-start = ((), (), s32[]{:S(2)}) async-start(), calls=%async_computation.9 | async-start | bytes 1474560 | tf_op jit(solution)/shard_map/all_gather | solution.py:116
  9.4 77.4 %all-gather.14.cloned.1.call-start = ((), (), s32[]{:S(2)}) async-start(), calls=%async_computation.10 | async-start | bytes 1474560 | tf_op jit(solution)/shard_map/all_gather | solution.py:118
  10.0 115.7 %all-gather.16.cloned.1.call-start = ((), (), s32[]{:S(2)}) async-start(), calls=%async_computation.11 | async-start | bytes 5898240 | tf_op jit(solution)/shard_map/all_gather | solution.py:153
  10.6 13.6 %copy-start = (bf16[512,768]{1,0:T(8,128)(2,1)S(1)}, bf16[512,768]{1,0:T(8,128)(2,1)}, u32[]{:S(2)}) copy-start(bf16[512,768]{1,0:T(8,128)(2,1)} %param.18) | copy-start | bytes 2359300
  10.6 153.9 %all-gather.18.cloned.1.call-start = ((), (), s32[]{:S(2)}) async-start(), calls=%async_computation.12 | async-start | bytes 5898240 | tf_op jit(solution)/shard_map/all_gather | solution.py:154
  11.2 13.8 %copy-start.25 = (s32[512]{0:T(512)S(1)}, s32[512]{0:T(512)}, u32[]{:S(2)}) copy-start(s32[512]{0:T(512)} %param.22) | copy-start | bytes 6148
  11.2 192.4 %all-gather.20.cloned.1.call-start = ((), (), s32[]{:S(2)}) async-start(), calls=%async_computation.13 | async-start | bytes 5898240 | tf_op jit(solution)/shard_map/all_gather | solution.py:155
  12.0 282.3 %reduce-scatter.10.cloned.1.call-start = ((), (), s32[]{:S(2)}) async-start(), calls=%async_computation.15 | async-start | bytes 1474560 | tf_op jit(solution)/shard_map/reduce_scatter | solution.py:305
  90.6 74.0 %copy-start.2 = (bf16[512,768]{1,0:T(8,128)(2,1)}, bf16[512,768]{1,0:T(8,128)(2,1)S(1)}, u32[]{:S(2)}) copy-start(bf16[512,768]{1,0:T(8,128)(2,1)S(1)} %multiply_convert_fusion.5) | copy-start | bytes 2359300
  132.5 71.1 %copy-start.12 = (bf16[512,768]{1,0:T(8,128)(2,1)S(1)}, bf16[512,768]{1,0:T(8,128)(2,1)}, u32[]{:S(2)}) copy-start(bf16[512,768]{1,0:T(8,128)(2,1)} %param.19) | copy-start | bytes 2359300
  213.7 7.3 %copy-start.33 = (bf16[512,3072]{1,0:T(8,128)(2,1)}, bf16[512,3072]{1,0:T(8,128)(2,1)S(1)}, u32[]{:S(2)}) copy-start(bf16[512,3072]{1,0:T(8,128)(2,1)S(1)} %get-tuple-element.204) | copy-start | bytes 9437188
  213.7 7.3 %copy-start.32 = (bf16[512,3072]{1,0:T(8,128)(2,1)}, bf16[512,3072]{1,0:T(8,128)(2,1)S(1)}, u32[]{:S(2)}) copy-start(bf16[512,3072]{1,0:T(8,128)(2,1)S(1)} %get-tuple-element.203) | copy-start | bytes 9437188
  213.7 7.3 %copy-start.5 = (f32[512,768]{1,0:T(8,128)S(1)}, f32[512,768]{1,0:T(8,128)}, u32[]{:S(2)}) copy-start(f32[512,768]{1,0:T(8,128)} %copy-done.4) | copy-start | bytes 4718596
  213.7 7.3 %copy-start.8 = (bf16[768,3072]{1,0:T(8,128)(2,1)S(1)}, bf16[768,3072]{1,0:T(8,128)(2,1)}, u32[]{:S(2)}) copy-start(bf16[768,3072]{1,0:T(8,128)(2,1)} %all-gather.18.cloned.1.call-done) | copy-start | bytes 14155780
  264.2 54.6 %reduce-scatter.8.cloned.1.call-start = ((), (), s32[]{:S(2)}) async-start(), calls=%async_computation.14 | async-start | bytes 1474560 | tf_op jit(solution)/shard_map/reduce_scatter | solution.py:302
  267.2 79.6 %reduce-scatter.14.cloned.1.call-start = ((), (), s32[]{:S(2)}) async-start(), calls=%async_computation.17 | async-start | bytes 1474560 | tf_op jit(solution)/shard_map/reduce_scatter | solution.py:311
  270.2 105.4 %reduce-scatter.12.cloned.1.call-start = ((), (), s32[]{:S(2)}) async-start(), calls=%async_computation.16 | async-start | bytes 1474560 | tf_op jit(solution)/shard_map/reduce_scatter | solution.py:308
  273.5 152.4 %reduce-scatter.16.cloned.1.call-start = ((), (), s32[]{:S(2)}) async-start(), calls=%async_computation.18 | async-start | bytes 5898240 | tf_op jit(solution)/shard_map/reduce_scatter | solution.py:200
  279.8 196.7 %reduce-scatter.18.cloned.1.call-start = ((), (), s32[]{:S(2)}) async-start(), calls=%async_computation.19 | async-start | bytes 5898240 | tf_op jit(solution)/shard_map/reduce_scatter | solution.py:203
  286.2 240.7 %reduce-scatter.20.cloned.1.call-start = ((), (), s32[]{:S(2)}) async-start(), calls=%async_computation.20 | async-start | bytes 5898240 | tf_op jit(solution)/shard_map/reduce_scatter | solution.py:206
  294.2 407.3 %all-reduce.10.cloned.1.call-start = ((), (), s32[]{:S(2)}) async-start(), calls=%async_computation.21 | async-start | bytes 9437184 | tf_op jit(solution)/shard_map/psum | solution.py:317
  531.6 33.5 %copy-start.23 = (f32[512]{0:T(512)S(1)}, f32[512]{0:T(512)}, u32[]{:S(2)}) copy-start(f32[512]{0:T(512)} %get-tuple-element.222) | copy-start | bytes 6148
  (28 other events, 59.9 us)
Sparse Core Ops, SparseCore 0:
  9.5 20.1 all-gather.7
  31.3 17.5 all-gather.9
  50.4 17.4 all-gather.11
  69.3 17.4 all-gather.13
  88.2 37.4 all-gather.15
  127.1 37.4 all-gather.17
  166.1 37.4 all-gather.19
  264.3 25.6 reduce-scatter.9
  293.1 25.6 reduce-scatter.7
  321.1 25.6 reduce-scatter.13
  349.9 25.6 reduce-scatter.11
  378.0 47.9 reduce-scatter.15
  428.5 47.9 reduce-scatter.17
  478.9 47.9 reduce-scatter.19
  531.3 170.1 all-reduce.9
where the time goes:
time: 728 us; the launch traced here: 718 us
  waiting for transfers between devices  499 us (69%)
  matrix products  122 us (17%)
  blocking collectives  37.4 us (5%)
  other arithmetic  28.5 us (4%)
  between operations  16.2 us (2%)
  local copies, waits for them, and re-layouts  13.7 us (2%)
    psum x1, waiting for transfers between devices, per_device(): lax.psum(attn_shares[1].astype(jnp.bfloat16), 'replica').astype(jnp.float32)  127 us
    reduce_scatter x1, waiting for transfers between devices, per_device(): lax.psum_scatter(ffn_terms[2].astype(jnp.bfloat16), 'shard', scatter_dime...  50.5 us
    reduce_scatter x1, waiting for transfers between devices, per_device(): lax.psum_scatter(ffn_terms[1].astype(jnp.bfloat16), 'shard', scatter_dime...  50.4 us
    reduce_scatter x1, waiting for transfers between devices, per_device(): lax.psum_scatter(ffn_terms[3].astype(jnp.bfloat16), 'shard', scatter_dime...  50.4 us
    all_gather x1, waiting for transfers between devices, per_device(): lax.all_gather(gate_weight, 'shard', axis=0, tiled=True)  35.1 us
    all_gather x1, waiting for transfers between devices, per_device(): lax.all_gather(down_weight, 'shard', axis=0, tiled=True)  32.2 us
    all_gather x1, waiting for transfers between devices, per_device(): lax.all_gather(up_weight, 'shard', axis=0, tiled=True)  32.1 us
    reduce_scatter x1, waiting for transfers between devices, per_device(): lax.psum_scatter(attn_terms[3].astype(jnp.bfloat16), 'shard', scatter_dim...  28.8 us
  transfers between devices with their start and end apart: 15, of which 14 were waited for; matrix products, arithmetic and copies ran while one was open for 13% of the time, Pallas kernels for 0%

commit v1 on v0

v1 whole, which is shorter than its diff:
```python
import functools
import math

import jax
import jax.numpy as jnp
from jax import lax
from jax.experimental import pallas as pl
from jax.experimental.pallas import tpu as pltpu
from jax.sharding import PartitionSpec as P

HEADS = 12
HDIM = 64
EPSILON = 1e-05
ROPE_BASE = 10000.0
MESH = pl.DeviceIdType.MESH
F32 = jnp.float32
BF16 = jnp.bfloat16
DMA = pltpu.SemaphoreType.DMA

ROWS = 192
COLS = 768
UNITS = 16
FBLOCKS = 4
SHARDS = 4
TILE = 256


def toggle(index, stride):
    return index + (1 - 2 * ((index // stride) % 2)) * stride


def ring(index, members, stride):
    place = (index // stride) % members
    base = index - place * stride
    return place, [base + ((place + step) % members) * stride for step in range(1, members)]


def at(shard, replica):
    return {"shard": shard, "replica": replica}


def greet(peers):
    barrier = pltpu.get_barrier_semaphore()
    for peer in peers:
        pl.semaphore_signal(barrier, inc=1, device_id=peer, device_id_type=MESH)
    pl.semaphore_wait(barrier, len(peers))


def remote(source, target, send, receive, peer):
    return pltpu.make_async_remote_copy(
        src_ref=source,
        dst_ref=target,
        send_sem=send,
        recv_sem=receive,
        device_id=peer,
        device_id_type=MESH,
    )


def mult(start, step):
    return start if isinstance(start, int) else pl.multiple_of(start, step)


def span(start, size, step=16):
    return pl.ds(mult(start, step), size)


def replica_factors(count):
    if count == 8:
        return [(2, 1), (4, 2)], 1
    assert count == 32
    return [(2, 16), (4, 4), (4, 1)], 4


def dot(a, b):
    return jnp.dot(a, b, preferred_element_type=F32)


def dot_nt(a, b):
    return lax.dot_general(a, b, (((1,), (1,)), ((), ())), preferred_element_type=F32)


def dot_tn(a, b):
    return lax.dot_general(a, b, (((0,), (0,)), ((), ())), preferred_element_type=F32)


def flat(block):
    return block.reshape(-1, block.shape[-1])


def scale_of(values):
    return lax.rsqrt(jnp.mean(values * values, axis=-1, keepdims=True) + EPSILON)


def half_swap(values):
    lane = lax.broadcasted_iota(jnp.int32, values.shape, 1)
    return jnp.where(lane % 64 < 32, pltpu.roll(values, 96, 1), pltpu.roll(values, 32, 1))


def head_mask(which):
    lane = lax.broadcasted_iota(jnp.int32, (1, 128), 1)
    return jnp.where((lane < 64) == (which == 0), 1.0, 0.0).astype(BF16)


def norm_back(grad_normed, values, gain):
    scale = scale_of(values)
    scaled = gain * grad_normed
    gain_grad = jnp.sum(grad_normed * values * scale, axis=0, keepdims=True)
    mean = jnp.mean(scaled * values, axis=-1, keepdims=True)
    return gain_grad, scale * scaled - values * (scale * scale * scale) * mean


def forward_kernel(
    length, x_hbm, tables_hbm, gain_hbm, q_hbm, k_hbm, v_hbm, o_hbm, g_hbm, u_hbm, d_hbm,
    w_out, qkv_out, nt_out, n2t_out, at_out, ht_out, hid_out, a_out, b_out, h1_out, lse_out, gain_out,
    w, x, tables, gains, gain, normed, normed_t, qkv, bias, attended, lse, h1, ht, hid, a, b,
    load, x_out, x_in, y_out, y_in, p_out, p_in, f_out, f_in, g_out, g_in, w_store, store, f_store,
):
    shard, replica = lax.axis_index("shard"), lax.axis_index("replica")
    partner, across = toggle(shard, 1), toggle(shard, 2)
    opposite = toggle(across, 1)
    beside = toggle(replica, 1)
    side = replica % 2
    tokens, width = x.shape

    sources = [q_hbm, k_hbm, v_hbm, o_hbm]
    for block in range(FBLOCKS):
        columns = pl.ds(block * COLS, COLS)
        sources += [g_hbm.at[:, columns], u_hbm.at[:, columns]]
    sources += [d_hbm.at[pl.ds(piece * ROWS, ROWS)] for piece in range(UNITS - len(sources))]
    loads = [
        pltpu.make_async_copy(source, w.at[unit, shard], load.at[unit])
        for unit, source in enumerate(sources)
    ]
    x_load = pltpu.make_async_copy(x_hbm, x, load.at[UNITS])
    gain_load = pltpu.make_async_copy(gain_hbm, gains.at[shard], load.at[UNITS + 1])
    table_load = pltpu.make_async_copy(tables_hbm, tables, load.at[UNITS + 2])
    gain_load.start()
    for copy in loads:
        copy.start()
    x_load.start()
    table_load.start()

    shard_peers = [at(partner, replica), at(across, replica), at(opposite, replica)]
    greet(shard_peers + [at(shard, beside)])

    gain_load.wait()
    gain_copies = [
        remote(gains.at[shard], gains.at[shard], g_out.at[number], g_in.at[number], peer)
        for number, peer in enumerate(shard_peers)
    ]
    for copy in gain_copies:
        copy.start()

    half = ROWS // 2

    def part(unit, owner, which):
        return w.at[unit, owner, span(which * half, half)]

    def cross(unit):
        piece = part(unit, shard, side)
        return remote(piece, piece, x_out.at[unit], x_in.at[unit], at(across, replica))

    def share(unit):
        piece = w.at[unit, shard]
        return remote(piece, piece, p_out.at[unit], p_in.at[unit], at(partner, replica))

    def hand(unit):
        piece = part(unit, across, side)
        return remote(piece, piece, y_out.at[unit], y_in.at[unit], at(shard, beside))

    def forward(unit, number):
        piece = part(unit, across, side if number == 0 else 1 - side)
        return remote(piece, piece, f_out.at[number, unit], f_in.at[number, unit], at(partner, replica))

    def keep(unit):
        return pltpu.make_async_copy(w.at[unit], w_out.at[unit], w_store.at[unit])

    for unit in range(UNITS):
        loads[unit].wait()
        cross(unit).start()
        share(unit).start()

    def tick(time):
        @pl.when(time < UNITS)
        def _():
            cross(time).wait_recv()
            hand(time).start()
            forward(time, 0).start()

        @pl.when((time >= 1) & (time < UNITS + 1))
        def _():
            hand(time - 1).wait_recv()
            forward(time - 1, 1).start()

        @pl.when((time >= 2) & (time < UNITS + 2))
        def _():
            unit = time - 2
            share(unit).wait_recv()
            forward(unit, 0).wait_recv()
            forward(unit, 1).wait_recv()
            keep(unit).start()

    def ticks(first, last):
        def body(time, carry):
            tick(time)
            return carry

        lax.fori_loop(first, last, body, 0)

    stores = []

    def save(source, target):
        copy = pltpu.make_async_copy(source, target, store.at[len(stores)])
        copy.start()
        stores.append(copy)

    row = lax.broadcasted_iota(jnp.int32, (tokens, tokens), 0)
    column = lax.broadcasted_iota(jnp.int32, (tokens, tokens), 1)
    seen = (column <= row) & ((row < length[0]) | (column >= length[0]))
    bias[...] = jnp.where(seen, 0.0, -jnp.inf)

    x_load.wait()
    for copy in gain_copies:
        copy.wait_recv()
    gain[...] = gains[0] + gains[1] + gains[2] + gains[3]
    save(gain, gain_out)
    values = x[...].astype(F32)
    normed[...] = (values * scale_of(values) * gain[0:1]).astype(BF16)
    normed_t[0] = normed[...].T
    save(normed_t.at[0], nt_out)
    table_load.wait()
    ticks(0, 5)

    def project(step, carry):
        which, tile = step // (tokens // TILE), step % (tokens // TILE)
        rows = span(tile * TILE, TILE)
        product = dot(normed[rows], flat(w[which]))
        cosine = jnp.where(which < 2, tables[0, rows], 1.0)
        sine = jnp.where(which < 2, tables[1, rows], 0.0)
        for pair in range(width // 128):
            columns = slice(pair * 128, pair * 128 + 128)
            piece = product[:, columns]
            qkv[which, rows, columns] = (piece * cosine + half_swap(piece) * sine).astype(BF16)
        return carry

    lax.fori_loop(0, 3 * (tokens // TILE), project, 0)
    save(qkv, qkv_out)
    lse[...] = jnp.zeros_like(lse)

    def attend(pair, carry):
        columns = span(pair * 128, 128, 128)
        for tile in range(tokens // TILE):
            rows = pl.ds(tile * TILE, TILE)
            keys = (tile + 1) * TILE
            query = qkv[0, rows, columns]
            key = qkv[1, 0:keys, columns]
            value = qkv[2, 0:keys, columns]
            mixed = []
            logs = lse[rows]
            lane = lax.broadcasted_iota(jnp.int32, logs.shape, 1)
            for which in range(2):
                scores = dot_nt(query * head_mask(which), key) * (1.0 / math.sqrt(HDIM))
                scores = scores + bias[rows, 0:keys]
                peak = jnp.max(scores, axis=-1, keepdims=True)
                exponent = jnp.exp(scores - peak)
                total = jnp.sum(exponent, axis=-1, keepdims=True)
                probability = (exponent * (1.0 / total)).astype(BF16)
                mixed.append(dot(probability, value))
                logs = jnp.where(lane == 2 * pair + which, peak + jnp.log(total), logs)
            lse[rows] = logs
            first = lax.broadcasted_iota(jnp.int32, mixed[0].shape, 1) < 64
            attended[rows, columns] = jnp.where(first, mixed[0], mixed[1]).astype(BF16)
        tick(5 + pair)
        return carry

    lax.fori_loop(0, HEADS // 2, attend, 0)
    normed_t[1] = attended[...].T
    save(normed_t.at[1], at_out)
    save(lse, lse_out)
    for tile in range(tokens // TILE):
        rows = pl.ds(tile * TILE, TILE)
        hidden_one = x[rows].astype(F32) + dot(attended[rows], flat(w[3]))
        h1[rows] = hidden_one
        normed[rows] = (hidden_one * scale_of(hidden_one) * gain[1:2]).astype(BF16)
    save(h1, h1_out)
    normed_t[2] = normed[...].T
    save(normed_t.at[2], n2t_out)

    def f_copies(block):
        pairs = [
            (hid.at[block], hid_out.at[block]),
            (a.at[block], a_out.at[block]),
            (b.at[block], b_out.at[block]),
            (ht.at[:, block], ht_out.at[:, block]),
        ]
        return [
            pltpu.make_async_copy(source, target, f_store.at[block, number])
            for number, (source, target) in enumerate(pairs)
        ]

    def feed(block, carry):
        def rows_of(tile, inner):
            rows = span(tile * TILE, TILE)
            gate = dot(normed[rows], flat(w[4 + 2 * block]))
            upward = dot(normed[rows], flat(w[5 + 2 * block]))
            sigmoid = jax.nn.sigmoid(gate)
            activated = gate * sigmoid
            hid[block, rows] = (activated * upward).astype(BF16)
            a[block, rows] = (upward * sigmoid * (1.0 + gate * (1.0 - sigmoid))).astype(BF16)
            b[block, rows] = activated.astype(BF16)
            return inner

        lax.fori_loop(0, tokens // TILE, rows_of, 0)
        turned = hid[block].T
        for piece in range(FBLOCKS):
            ht[piece, block] = turned[piece * ROWS : (piece + 1) * ROWS]
        for copy in f_copies(block):
            copy.start()
        tick(11 + block)
        return carry

    lax.fori_loop(0, FBLOCKS, feed, 0)
    ticks(11 + FBLOCKS, UNITS + 2)

    def settle(unit, carry):
        cross(unit).wait_send()
        share(unit).wait_send()
        hand(unit).wait_send()
        forward(unit, 0).wait_send()
        forward(unit, 1).wait_send()
        keep(unit).wait()
        return carry

    lax.fori_loop(0, UNITS, settle, 0)
    for copy in gain_copies:
        copy.wait_send()
    for copy in stores:
        copy.wait()
    for block in range(FBLOCKS):
        for copy in f_copies(block):
            copy.wait()


def forward_pass(length, tokens, tables, gain_rows, weights):
    count, width = tokens.shape
    shape = jax.ShapeDtypeStruct
    outs = (
        shape((UNITS, SHARDS, ROWS, COLS), BF16),
        shape((3, count, width), BF16),
        shape((width, count), BF16),
        shape((width, count), BF16),
        shape((width, count), BF16),
        shape((FBLOCKS, FBLOCKS, ROWS, count), BF16),
        shape((FBLOCKS, count, COLS), BF16),
        shape((FBLOCKS, count, COLS), BF16),
        shape((FBLOCKS, count, COLS), BF16),
        shape((count, width), F32),
        shape((count, 128), F32),
        shape(gain_rows.shape, F32),
    )
    anywhere = pl.BlockSpec(memory_space=pl.ANY)
    return pl.pallas_call(
        forward_kernel,
        out_shape=outs,
        in_specs=[pl.BlockSpec(memory_space=pltpu.SMEM)] + [anywhere] * 10,
        out_specs=[anywhere] * len(outs),
        scratch_shapes=[
            pltpu.VMEM((UNITS, SHARDS, ROWS, COLS), BF16),
            pltpu.VMEM((count, width), BF16),
            pltpu.VMEM(tables.shape, F32),
            pltpu.VMEM((SHARDS,) + gain_rows.shape, F32),
            pltpu.VMEM(gain_rows.shape, F32),
            pltpu.VMEM((count, width), BF16),
            pltpu.VMEM((3, width, count), BF16),
            pltpu.VMEM((3, count, width), BF16),
            pltpu.VMEM((count, count), F32),
            pltpu.VMEM((count, width), BF16),
            pltpu.VMEM((count, 128), F32),
            pltpu.VMEM((count, width), F32),
            pltpu.VMEM((FBLOCKS, FBLOCKS, ROWS, count), BF16),
            pltpu.VMEM((FBLOCKS, count, COLS), BF16),
            pltpu.VMEM((FBLOCKS, count, COLS), BF16),
            pltpu.VMEM((FBLOCKS, count, COLS), BF16),
            DMA((UNITS + 3,)),
            DMA((UNITS,)), DMA((UNITS,)), DMA((UNITS,)), DMA((UNITS,)), DMA((UNITS,)), DMA((UNITS,)),
            DMA((2, UNITS)), DMA((2, UNITS)), DMA((3,)), DMA((3,)),
            DMA((UNITS,)), DMA((8,)), DMA((FBLOCKS, 4)),
        ],
        compiler_params=pltpu.CompilerParams(
            collective_id=0, has_side_effects=True, vmem_limit_bytes=60 * 1024 * 1024
        ),
        name="forward_gather",
    )(length, tokens, tables, gain_rows, *weights)


def backward_kernel(
    factors, pack,
    length, x_hbm, cot_hbm, tables_hbm, gain_hbm, w_hbm, qkv_hbm, nt_hbm, n2t_hbm, at_hbm, ht_hbm,
    hid_hbm, a_hbm, b_hbm, h1_hbm, lse_hbm,
    sums_out, gain_out, output_out, grad_out,
    *refs,
):
    levels = len(factors)
    (grads, near, far, gain_sum, gain_got, x, gbt, gain, turned, h1, acc, result, out_low) = refs[:13]
    parts = refs[13 : 13 + levels]
    sems = refs[13 + levels :]
    load, s_load, near_out, near_in, far_out, far_in, store, gain_send, gain_recv = sems[:9]
    down_out, down_in, up_out, up_in = (
        sems[9 + kind * levels : 9 + (kind + 1) * levels] for kind in range(4)
    )
    shard, replica = lax.axis_index("shard"), lax.axis_index("replica")
    partner, across = toggle(shard, 1), toggle(shard, 2)
    opposite = toggle(across, 1)
    tokens, width = x.shape
    groups = [ring(replica, members, stride) for members, stride in factors]
    flips = [at(partner, replica), at(across, replica)]
    stride, replicas = 1, math.prod(members for members, _ in factors)
    while stride < replicas:
        flips.append(at(shard, toggle(replica, stride)))
        stride *= 2

    def fetch(source, target, number):
        copy = pltpu.make_async_copy(source, target, load.at[number])
        copy.start()
        return copy

    cot_load = fetch(cot_hbm, gbt, 0)
    n2t_load = fetch(n2t_hbm, turned.at[0], 1)
    h1_load = fetch(h1_hbm, h1, 2)
    x_load = fetch(x_hbm, x, 3)
    gain_load = fetch(gain_hbm, gain, 4)
    at_load = fetch(at_hbm, turned.at[1], 5)
    nt_load = fetch(nt_hbm, turned.at[2], 6)

    greet(
        [at(partner, replica), at(across, replica)]
        + [at(shard, other) for _, others in groups for other in others]
    )

    chunks = UNITS // pack

    def region(chunk, places):
        unit, units, row, rows, column, columns = chunk * pack, pack, 0, ROWS, 0, COLS
        for level, place in enumerate(places):
            if level == levels - 1:
                rows, columns = rows // 2, columns // 2
                row = row + (place // 2) * rows
                column = column + (place % 2) * columns
                continue
            members = factors[level][0]
            by_unit = math.gcd(units, members)
            by_row = members // by_unit
            units, rows = units // by_unit, rows // by_row
            unit = unit + (place // by_row) * units
            row = row + (place % by_row) * rows
        return pl.ds(unit, units), span(row, rows), span(column, columns, 128)

    my_places = [place for place, _ in groups]

    def view(owner, chunk, places):
        units, rows, columns = region(chunk, places)
        return grads.at[units, owner, rows, columns]

    def near_copy(unit, which):
        return remote(
            grads.at[unit, opposite if which == 0 else partner],
            near.at[unit, which],
            near_out.at[unit, which],
            near_in.at[unit, which],
            at(partner, replica),
        )

    def far_copy(unit):
        return remote(
            grads.at[unit, across], far.at[unit], far_out.at[unit], far_in.at[unit], at(across, replica)
        )

    def down_copy(level, chunk, step):
        members = factors[level][0]
        place, others = groups[level]
        theirs = (place + step + 1) % members
        return remote(
            view(shard, chunk, my_places[:level] + [theirs]),
            parts[level].at[chunk, step],
            down_out[level].at[chunk, step],
            down_in[level].at[chunk, step],
            at(shard, others[step]),
        )

    def up_copy(level, chunk, step):
        piece = view(partner, chunk, my_places[: level + 1])
        return remote(
            piece,
            piece,
            up_out[level].at[chunk, step],
            up_in[level].at[chunk, step],
            at(shard, groups[level][1][step]),
        )

    def store_copy(chunk):
        units = pl.ds(chunk * pack, pack)
        return pltpu.make_async_copy(grads.at[units, partner], sums_out.at[units], store.at[chunk])

    def over(level, act):
        for step in range(factors[level][0] - 1):
            act(step)

    def give(unit):
        for which in range(2):
            near_copy(unit, which).start()

    def plus(*terms):
        total = terms[0].astype(F32)
        for term in terms[1:]:
            total = total + term.astype(F32)
        return total.astype(BF16)

    def take_near(unit):
        near_copy(unit, 0).wait_recv()
        grads[unit, across] = plus(grads[unit, across], near[unit, 0])
        far_copy(unit).start()
        near_copy(unit, 1).wait_recv()
        grads[unit, shard] = plus(grads[unit, shard], near[unit, 1])

    def take_far(chunk):
        for piece in range(pack):
            unit = chunk * pack + piece
            near_copy(unit, 0).wait_send()
            near_copy(unit, 1).wait_send()
            far_copy(unit).wait_recv()
            grads[unit, shard] = plus(grads[unit, shard], far[unit])
        over(0, lambda step: down_copy(0, chunk, step).start())

    def take_down(level, chunk):
        over(level, lambda step: down_copy(level, chunk, step).wait_recv())
        places = my_places[: level + 1]
        terms = [view(shard, chunk, places)[...]]
        terms += [parts[level][chunk, step] for step in range(factors[level][0] - 1)]
        total = plus(*terms)
        if level + 1 < levels:
            view(shard, chunk, places)[...] = total
            over(level + 1, lambda step: down_copy(level + 1, chunk, step).start())
        else:
            view(partner, chunk, places)[...] = total
            over(level, lambda step: up_copy(level, chunk, step).start())

    def take_up(level, chunk):
        over(level, lambda step: up_copy(level, chunk, step).wait_recv())
        if level > 0:
            over(level - 1, lambda step: up_copy(level - 1, chunk, step).start())
        else:
            store_copy(chunk).start()

    stages = [take_far]
    stages += [functools.partial(take_down, level) for level in range(levels)]
    stages += [functools.partial(take_up, level) for level in reversed(range(levels))]
    last_post = pack * (chunks + len(stages) - 1)

    def post(time):
        step = (time + 1) // pack - 1
        for lag, stage in enumerate(stages):
            good = (step >= lag) & (step < chunks + lag) & ((time + 1) % pack == 0)
            pl.when(good)(functools.partial(stage, step - lag))

    def posts(first, last):
        def body(time, carry):
            post(time)
            return carry

        lax.fori_loop(first, last, body, 0)

    def gain_copy(step):
        return remote(
            gain_sum.at[step], gain_got.at[step], gain_send.at[step], gain_recv.at[step], flips[step]
        )

    row = lax.broadcasted_iota(jnp.int32, (tokens, 1), 0)
    valid = jnp.where(row < length[0], 1.0, 0.0)

    def feed_forward(ht, down_w, gate_w, up_w, hid, a, b, grad_pair):
        def stream(block):
            slot = block % 2
            pairs = [
                (w_hbm.at[pl.ds(UNITS - FBLOCKS, FBLOCKS), block], down_w.at[slot]),
                (w_hbm.at[4 + 2 * block], gate_w.at[slot]),
                (w_hbm.at[5 + 2 * block], up_w.at[slot]),
                (hid_hbm.at[block], hid.at[slot]),
                (a_hbm.at[block], a.at[slot]),
                (b_hbm.at[block], b.at[slot]),
            ]
            return [
                pltpu.make_async_copy(source, target, s_load.at[slot, number])
                for number, (source, target) in enumerate(pairs)
            ]

        ht_load = fetch(ht_hbm, ht, 7)
        for copy in stream(0):
            copy.start()
        cot_load.wait()
        gbt[...] = (gbt[...].astype(F32) * valid).astype(BF16)
        ht_load.wait()

        def down_grads(unit, carry):
            for owner in range(SHARDS // 2):
                pair = pl.ds(2 * owner, 2)
                product = dot(flat(ht[unit, pair]), gbt[...]).astype(BF16)
                grads[unit, pair] = product.reshape(2, ROWS, COLS)
            give(unit)
            return carry

        lax.fori_loop(0, FBLOCKS, down_grads, 0)
        n2t_load.wait()
        acc[...] = jnp.zeros_like(acc)
        result[...] = jnp.zeros_like(result)

        def block_step(block, carry):
            slot = block % 2

            @pl.when(block + 1 < FBLOCKS)
            def _():
                for copy in stream(block + 1):
                    copy.start()

            for copy in stream(block):
                copy.wait()

            def rows_of(tile, inner):
                rows = span(tile * TILE, TILE)
                grad_hidden = dot_nt(gbt[rows], flat(down_w[slot]))
                grad_pair[0, rows] = (grad_hidden * a[slot, rows].astype(F32)).astype(BF16)
                grad_pair[1, rows] = (grad_hidden * b[slot, rows].astype(F32)).astype(BF16)
                return inner

            lax.fori_loop(0, tokens // TILE, rows_of, 0)
            pl.when(block == 0)(lambda: take_near(0))

            def kind_of(kind, inner):
                unit = FBLOCKS + 2 * block + kind
                for owner in range(SHARDS // 2):
                    pair = pl.ds(2 * owner, 2)
                    product = dot(
                        turned[0, pl.ds(2 * owner * ROWS, 2 * ROWS)], grad_pair[kind]
                    ).astype(BF16)
                    grads[unit, pair] = product.reshape(2, ROWS, COLS)
                give(unit)
                return inner

            lax.fori_loop(0, 2, kind_of, 0)

            @pl.when(block == 0)
            def _():
                for unit in range(1, FBLOCKS):
                    take_near(unit)

            def back_rows(tile, inner):
                rows = span(tile * TILE, TILE)
                acc[rows] += dot_nt(grad_pair[0, rows], flat(gate_w[slot])) + dot_nt(
                    grad_pair[1, rows], flat(up_w[slot])
                )
                result[rows] += dot(hid[slot, rows], flat(down_w[slot]))
                return inner

            lax.fori_loop(0, tokens // TILE, back_rows, 0)
            take_near(FBLOCKS + 2 * block)
            take_near(FBLOCKS + 2 * block + 1)
            post(block)
            return carry

        lax.fori_loop(0, FBLOCKS, block_step, 0)

    pl.run_scoped(
        feed_forward,
        pltpu.VMEM((FBLOCKS, FBLOCKS, ROWS, tokens), BF16),
        pltpu.VMEM((2, FBLOCKS, ROWS, COLS), BF16),
        pltpu.VMEM((2, SHARDS, ROWS, COLS), BF16),
        pltpu.VMEM((2, SHARDS, ROWS, COLS), BF16),
        pltpu.VMEM((2, tokens, COLS), BF16),
        pltpu.VMEM((2, tokens, COLS), BF16),
        pltpu.VMEM((2, tokens, COLS), BF16),
        pltpu.VMEM((2, tokens, COLS), BF16),
    )

    def attention(attn_w, tables, qkv, lse, bias, grad_attended, grad_qkv):
        w_load = fetch(w_hbm.at[pl.ds(0, 4)], attn_w, 8)
        qkv_load = fetch(qkv_hbm, qkv, 9)
        lse_load = fetch(lse_hbm, lse, 10)
        table_load = fetch(tables_hbm, tables, 11)
        h1_load.wait()
        gain_load.wait()

        gain_grad = jnp.zeros((1, width), F32)
        for tile in range(tokens // TILE):
            rows = pl.ds(tile * TILE, TILE)
            good = jnp.where(
                lax.broadcasted_iota(jnp.int32, (TILE, 1), 0) + tile * TILE < length[0], 1.0, 0.0
            )
            out_low[rows] = ((h1[rows] + result[rows]) * good).astype(BF16)
            gain_piece, back = norm_back(acc[rows], h1[rows], gain[1:2])
            gain_grad = gain_grad + gain_piece
            grad_one = gbt[rows].astype(F32) + back
            result[rows] = grad_one
            gbt[rows] = grad_one.astype(BF16)
        gain_sum[0] = jnp.zeros_like(gain_sum[0])
        gain_sum[0, 1:2] = gain_grad
        output_store = pltpu.make_async_copy(out_low, output_out, load.at[12])
        output_store.start()
        at_load.wait()
        for owner in range(SHARDS // 2):
            pair = pl.ds(2 * owner, 2)
            product = dot(turned[1, pl.ds(2 * owner * ROWS, 2 * ROWS)], gbt[...]).astype(BF16)
            grads[UNITS - 4, pair] = product.reshape(2, ROWS, COLS)
        give(UNITS - 4)
        w_load.wait()
        for tile in range(tokens // TILE):
            rows = pl.ds(tile * TILE, TILE)
            grad_attended[rows] = dot_nt(gbt[rows], flat(attn_w[3])).astype(BF16)
        take_near(UNITS - 4)
        post(FBLOCKS)

        key_row = lax.broadcasted_iota(jnp.int32, (tokens, tokens), 0)
        query_column = lax.broadcasted_iota(jnp.int32, (tokens, tokens), 1)
        seen = (key_row <= query_column) & ((query_column < length[0]) | (key_row >= length[0]))
        bias[...] = jnp.where(seen, 0.0, -jnp.inf)
        qkv_load.wait()
        lse_load.wait()
        table_load.wait()
        inv_root = 1.0 / math.sqrt(HDIM)

        def attend_back(pair, carry):
            columns = span(pair * 128, 128, 128)
            grad_key = [jnp.zeros((TILE, 128), F32) for _ in range(tokens // TILE)]
            grad_value = [jnp.zeros((TILE, 128), F32) for _ in range(tokens // TILE)]
            for tile in range(tokens // TILE):
                rows = pl.ds(tile * TILE, TILE)
                query = qkv[0, rows, columns]
                grad_mixed = grad_attended[rows, columns]
                grad_query = jnp.zeros((TILE, 128), F32)
                for which in range(2):
                    mask = head_mask(which)
                    query_one = query * mask
                    mixed_one = grad_mixed * mask
                    log_row = lse[2 * pair + which, :, rows]
                    probs, grad_probs = [], []
                    row_dot = jnp.zeros((1, TILE), F32)
                    for block in range(tile + 1):
                        keys = pl.ds(block * TILE, TILE)
                        scores = dot_nt(qkv[1, keys, columns], query_one) * inv_root
                        prob = jnp.exp(scores + bias[keys, rows] - log_row)
                        grad_value[block] += dot(prob.astype(BF16), mixed_one)
                        grad_prob = dot_nt(qkv[2, keys, columns], mixed_one)
                        row_dot = row_dot + jnp.sum(prob * grad_prob, axis=0, keepdims=True)
                        probs.append(prob)
                        grad_probs.append(grad_prob)
                    for block in range(tile + 1):
                        keys = pl.ds(block * TILE, TILE)
                        grad_scores = (probs[block] * (grad_probs[block] - row_dot)).astype(BF16)
                        grad_key[block] += dot(grad_scores, query_one)
                        grad_query += dot_tn(grad_scores, qkv[1, keys, columns] * mask)
                grad_query = grad_query * inv_root
                grad_query = grad_query * tables[0, rows] - half_swap(grad_query) * tables[1, rows]
                grad_qkv[0, rows, columns] = grad_query.astype(BF16)
            for block in range(tokens // TILE):
                keys = pl.ds(block * TILE, TILE)
                back = grad_key[block] * inv_root
                back = back * tables[0, keys] - half_swap(back) * tables[1, keys]
                grad_qkv[1, keys, columns] = back.astype(BF16)
                grad_qkv[2, keys, columns] = grad_value[block].astype(BF16)
            post(FBLOCKS + 1 + pair)
            return carry

        lax.fori_loop(0, HEADS // 2, attend_back, 0)
        nt_load.wait()

        def projection(which, carry):
            for owner in range(SHARDS // 2):
                pair = pl.ds(2 * owner, 2)
                product = dot(
                    turned[2, pl.ds(2 * owner * ROWS, 2 * ROWS)], grad_qkv[which]
                ).astype(BF16)
                grads[UNITS - 3 + which, pair] = product.reshape(2, ROWS, COLS)
            give(UNITS - 3 + which)
            return carry

        lax.fori_loop(0, 3, projection, 0)
        acc[...] = jnp.zeros_like(acc)

        def input_back(which, carry):
            for tile in range(tokens // TILE):
                rows = pl.ds(tile * TILE, TILE)
                acc[rows] += dot_nt(grad_qkv[which, rows], flat(attn_w[which]))
            take_near(UNITS - 3 + which)
            return carry

        lax.fori_loop(0, 3, input_back, 0)
        x_load.wait()
        gain_grad = jnp.zeros((1, width), F32)
        for tile in range(tokens // TILE):
            rows = pl.ds(tile * TILE, TILE)
            gain_piece, back = norm_back(acc[rows], x[rows].astype(F32), gain[0:1])
            gain_grad = gain_grad + gain_piece
            result[rows] = result[rows] + back
        gain_sum[0, 0:1] = gain_grad
        grad_store = pltpu.make_async_copy(result, grad_out, load.at[13])
        grad_store.start()
        output_store.wait()
        grad_store.wait()

    pl.run_scoped(
        attention,
        pltpu.VMEM((4, SHARDS, ROWS, COLS), BF16),
        pltpu.VMEM((2, tokens, 128), F32),
        pltpu.VMEM((3, tokens, width), BF16),
        pltpu.VMEM((HEADS, 1, tokens), F32),
        pltpu.VMEM((tokens, tokens), F32),
        pltpu.VMEM((tokens, width), BF16),
        pltpu.VMEM((3, tokens, width), BF16),
    )

    first = FBLOCKS + 1 + HEADS // 2
    gain_copy(0).start()

    def rest(time, carry):
        post(time)
        for step in range(len(flips)):

            @pl.when(time == first + 1 + step)
            def _():
                gain_copy(step).wait_recv()
                gain_sum[step + 1] = gain_sum[step] + gain_got[step]
                if step + 1 < len(flips):
                    gain_copy(step + 1).start()

        return carry

    assert first + 1 + len(flips) <= last_post
    lax.fori_loop(first, last_post, rest, 0)
    gain_out[...] = gain_sum[len(flips)]

    def settle(chunk, carry):
        for piece in range(pack):
            far_copy(chunk * pack + piece).wait_send()
        for level in range(levels):
            over(level, lambda step: down_copy(level, chunk, step).wait_send())
            over(level, lambda step: up_copy(level, chunk, step).wait_send())
        store_copy(chunk).wait()
        return carry

    lax.fori_loop(0, chunks, settle, 0)
    for step in range(len(flips)):
        gain_copy(step).wait_send()


def backward_pass(length, tokens, cotangent, tables, gain, saved):
    count, width = tokens.shape
    replicas = lax.axis_size("replica")
    factors, pack = replica_factors(replicas)
    levels = len(factors)
    chunks = UNITS // pack
    flips = 2 + replicas.bit_length() - 1
    part_shapes = []
    units, rows, columns = pack, ROWS, COLS
    for level, (members, _) in enumerate(factors):
        if level == levels - 1:
            rows, columns = rows // 2, columns // 2
        else:
            by_unit = math.gcd(units, members)
            units, rows = units // by_unit, rows // (members // by_unit)
        part_shapes.append((chunks, members - 1, units, rows, columns))
    counts = [(chunks, members - 1) for members, _ in factors]
    anywhere = pl.BlockSpec(memory_space=pl.ANY)
    shape = jax.ShapeDtypeStruct
    return pl.pallas_call(
        functools.partial(backward_kernel, factors, pack),
        out_shape=(
            shape((UNITS, ROWS, COLS), BF16),
            shape(gain.shape, F32),
            shape((count, width), BF16),
            shape((count, width), F32),
        ),
        in_specs=[pl.BlockSpec(memory_space=pltpu.SMEM)] + [anywhere] * (4 + len(saved)),
        out_specs=[anywhere, pl.BlockSpec(memory_space=pltpu.VMEM), anywhere, anywhere],
        scratch_shapes=[
            pltpu.VMEM((UNITS, SHARDS, ROWS, COLS), BF16),
            pltpu.VMEM((UNITS, 2, ROWS, COLS), BF16),
            pltpu.VMEM((UNITS, ROWS, COLS), BF16),
            pltpu.VMEM((flips + 1,) + gain.shape, F32),
            pltpu.VMEM((flips,) + gain.shape, F32),
            pltpu.VMEM((count, width), BF16),
            pltpu.VMEM((count, width), BF16),
            pltpu.VMEM(gain.shape, F32),
            pltpu.VMEM((3, width, count), BF16),
            pltpu.VMEM((count, width), F32),
            pltpu.VMEM((count, width), F32),
            pltpu.VMEM((count, width), F32),
            pltpu.VMEM((count, width), BF16),
        ]
        + [pltpu.VMEM(part, BF16) for part in part_shapes]
        + [
            DMA((14,)), DMA((2, 6)), DMA((UNITS, 2)), DMA((UNITS, 2)), DMA((UNITS,)), DMA((UNITS,)),
            DMA((chunks,)), DMA((flips,)), DMA((flips,)),
        ]
        + [DMA(count_) for _ in range(4) for count_ in counts],
        compiler_params=pltpu.CompilerParams(
            collective_id=1, has_side_effects=True, vmem_limit_bytes=67043328
        ),
        name="backward_reduce",
    )(length, tokens, cotangent, tables, gain, *saved)


def widen_kernel(units, *refs):
    outs, (low, wide, in_sem, out_sem) = refs[:7], refs[7:]
    down, gate, up, out, query, key, value = outs
    targets = [down.at[pl.ds(piece * ROWS, ROWS)] for piece in range(FBLOCKS)]
    for block in range(FBLOCKS):
        columns = pl.ds(block * COLS, COLS)
        targets += [gate.at[:, columns], up.at[:, columns]]
    targets += [out, query, key, value]
    ins = [
        pltpu.make_async_copy(units.at[unit], low.at[unit], in_sem.at[unit]) for unit in range(UNITS)
    ]
    puts = [
        pltpu.make_async_copy(wide.at[unit], target, out_sem.at[unit])
        for unit, target in enumerate(targets)
    ]
    for copy in ins:
        copy.start()
    for unit in range(UNITS):
        ins[unit].wait()
        wide[unit] = low[unit].astype(F32)
        puts[unit].start()
    for copy in puts:
        copy.wait()


def widen(units):
    shape = jax.ShapeDtypeStruct
    small, broad = shape((ROWS, COLS), F32), shape((ROWS, FBLOCKS * COLS), F32)
    anywhere = pl.BlockSpec(memory_space=pl.ANY)
    return pl.pallas_call(
        widen_kernel,
        out_shape=(shape((FBLOCKS * ROWS, COLS), F32), broad, broad, small, small, small, small),
        in_specs=[anywhere],
        out_specs=[anywhere] * 7,
        scratch_shapes=[
            pltpu.VMEM((UNITS, ROWS, COLS), BF16),
            pltpu.VMEM((UNITS, ROWS, COLS), F32),
            DMA((UNITS,)),
            DMA((UNITS,)),
        ],
        compiler_params=pltpu.CompilerParams(vmem_limit_bytes=24 * 1024 * 1024),
        name="widen",
    )(units)


def per_device(
    tokens, cotangent, lengths, assignment, positions, attention_gain, query_weight, key_weight,
    value_weight, out_weight, feedforward_gain, gate_weight, up_weight, down_weight,
):
    width = tokens.shape[1]
    share = attention_gain.shape[0]
    shard = lax.axis_index("shard")
    device = shard * lax.axis_size("replica") + lax.axis_index("replica")
    length = jnp.sum(jnp.where(assignment == device, lengths, 0)).reshape(1)

    half = HDIM // 2
    lane = jnp.arange(128)
    frequency = jnp.exp((lane % half).astype(F32) * (-2.0 * math.log(ROPE_BASE) / HDIM))
    angles = positions.astype(F32)[:, None] * frequency[None, :]
    sign = jnp.where(lane % HDIM < half, -1.0, 1.0)
    tables = jnp.stack([jnp.cos(angles), jnp.sin(angles) * sign[None, :]])

    gain_rows = jnp.stack([attention_gain, feedforward_gain]).astype(F32)
    gain_rows = lax.dynamic_update_slice(jnp.zeros((8, width), F32), gain_rows, (0, shard * share))

    w, qkv, nt, n2t, att, ht, hid, a, b, h1, lse, gain = forward_pass(
        length,
        tokens,
        tables,
        gain_rows,
        [query_weight, key_weight, value_weight, out_weight, gate_weight, up_weight, down_weight],
    )
    lse = lse[:, :HEADS].T.reshape(HEADS, 1, -1)
    sums, gain_sums, output, input_grad = backward_pass(
        length, tokens, cotangent, tables, gain, [w, qkv, nt, n2t, att, ht, hid, a, b, h1, lse]
    )
    down, gate, up, out, query, key, value = widen(sums)
    mine = lax.dynamic_slice(gain_sums, (0, shard * share), (2, share))
    return output, input_grad, mine[0], query, key, value, out, mine[1], gate, up, down


def solution(mesh):
    return jax.shard_map(
        per_device,
        mesh=mesh,
        in_specs=(
            P(("shard", "replica"), None),
            P(("shard", "replica"), None),
            P(),
            P(),
            P(("shard", "replica")),
            P("shard"),
            P("shard", None),
            P("shard", None),
            P("shard", None),
            P("shard", None),
            P("shard"),
            P("shard", None),
            P("shard", None),
            P("shard", None),
        ),
        out_specs=(
            P(("shard", "replica"), None),
            P(("shard", "replica"), None),
            P("shard"),
            P("shard", None),
            P("shard", None),
            P("shard", None),
            P("shard", None),
            P("shard"),
            P("shard", None),
            P("shard", None),
            P("shard", None),
        ),
        check_vma=False,
    )
```

time: 728 us -> 242 us (0.33); the launches traced: 718 us -> 242 us
  waiting for transfers between devices: 499 us -> 0 us
  Pallas kernels: 0 us -> 228 us
  matrix products: 122 us -> 0 us
  blocking collectives: 37.4 us -> 0 us
  other arithmetic: 28.5 us -> 3.83 us
  between operations: 16.2 us -> 0.74 us
    reduce_scatter x7 -> x0, waiting for transfers between devices: 233 us -> none  [the longest x1 50.5 us: per_device(): lax.psum_scatter(ffn_terms[2].astype(jnp.bfloat16), 'shard', scatter_dime...]
    pallas_call x0 -> x3, Pallas kernels: none -> 228 us  [the longest x1 149 us: backward_pass(): pl.pallas_call(functools.partial(backward_kernel, factors, pack), out_sha...]
    all_gather x7 -> x0, waiting for transfers between devices: 134 us -> none  [the longest x1 35.1 us: per_device(): lax.all_gather(gate_weight, 'shard', axis=0, tiled=True)]
    psum x1 -> x0, waiting for transfers between devices: 127 us -> none  [per_device(): lax.psum(attn_shares[1].astype(jnp.bfloat16), 'replica').astype(jnp.float32)]
    dot_general x42 -> x0, matrix products: 122 us -> none  [the longest x1 10.1 us: per_device(): jnp.einsum('nd,fd->nf', grad_branch_two, w_down, preferred_element_type=j...]
    psum x1 -> x0, blocking collectives: 23 us -> none  [per_device(): lax.psum(attn_shares[0].astype(jnp.bfloat16), 'replica').astype(jnp.float32)]
    convert_element_type x17 -> x2, other arithmetic: 15.4 us -> 0.7 us  [the longest x1 0.69 us: per_device(): angles = positions.astype(F32)[:, None] * frequency[None, :]]
    unnamed x2 -> x0, blocking collectives: 14.4 us -> none
  transfers between devices with their start and end apart: 15 -> 0, of which waited for: 14 -> 0; matrix products, arithmetic and copies ran while one was open for 13% -> 0% of each run, Pallas kernels for 0% -> 0%
where the time goes in v1:
time: 242 us
  Pallas kernels  228 us (94%)
  local copies, waits for them, and re-layouts  9.23 us (4%)
  other arithmetic  3.83 us (2%)
    pallas_call x1, Pallas kernels, backward_pass(): pl.pallas_call(functools.partial(backward_kernel, factors, pack), out_sha...  149 us
    pallas_call x1, Pallas kernels, forward_pass(): pl.pallas_call(forward_kernel, out_shape=outs, in_specs=[pl.BlockSpec(mem...  74.8 us
    pallas_call x1, Pallas kernels, widen(): pl.pallas_call(widen_kernel, out_shape=(shape((FBLOCKS * ROWS, COLS), F32...  4.89 us

profile of v1, /device:TPU:0, one launch (start us, length us, event | category | flops | bytes accessed | tf_op | source)
XLA Modules:
  0.0 242.1 jit_solution(9025448585523070634)
XLA Ops:
  0.6 0.7 stack.15
  1.3 0.7 stack.16
  2.0 0.4 dynamic_update_slice.3.gain_hbm
  2.4 0.0 copy-start.3
  2.4 0.7 convert_element_type.13
  3.1 1.0 multiply_cosine_fusion
  4.1 0.8 pad_maximum_fusion.tables_hbm
  4.9 1.3 fusion.1
  6.3 0.0 copy-done.3
  6.3 74.8 %forward_gather.1 = (bf16[16,4,192,768]{3,2,1,0:T(8,128)(2,1)}, bf16[3,512,768]{2,1,0:T(8,128)(2,1)}, bf16[768,512]{1,0:T(8,128)(2,1)}, bf16[768,512]{1,0:T(8,12...) custom-call(s32[1]{0:T(128)} %bitcast.length, ...), custom_call_target="tpu_custom_call" | custom-call | tf_op jit(solution)/shard_map/forward_gather/pallas_call | solution.py:363
  81.1 1.1 copy.25
  82.2 0.6 reshape.161.lse_hbm
  82.8 148.6 %backward_reduce.1 = (bf16[16,192,768]{2,1,0:T(8,128)(2,1)}, f32[8,768]{1,0:T(8,128)}, bf16[512,768]{1,0:T(8,128)(2,1)}, f32[512,768]{1,0:T(8,128)}) custom-call(s32[1]{0:T(128)} %bitcast.length, bf16[512,768]{1,0:T(8,128)(2,1)} %x_hbm.3, bf16[512,768]{1,0:T(8,128)(2,1)} %cot_hbm.1, f32[2,512,128]{2,1,0:T(8,128)} %pad_maximum_fusion.tables_hbm, ...), custom_call_target="tpu_custom_call" | custom-call | tf_op jit(solution)/shard_map/backward_reduce/pallas_call | solution.py:873
  231.4 0.0 copy-start
  231.4 2.3 copy-done
  233.8 0.0 copy-start.2
  233.8 0.0 copy-start.1
  233.8 4.9 %widen.1 = (f32[768,768]{1,0:T(8,128)}, f32[192,3072]{1,0:T(8,128)}, f32[192,3072]{1,0:T(8,128)}, f32[192,768]{1,0:T(8,128)}, f32[192,768]{1,0:T(8,128)}, /*index=5*/f32[192,768]{1,0:T(8,128)}, f32[192,768]{1,0:T(8,128)}) custom-call(bf16[16,192,768]{2,1,0:T(8,128)(2,1)S(1)} %copy-done), custom_call_target="tpu_custom_call" | custom-call | tf_op jit(solution)/shard_map/widen/pallas_call | solution.py:940
  238.7 1.4 fusion.5
  240.1 0.0 copy-done.2
  240.1 0.9 copy.29
  241.0 0.0 copy-done.1
  241.0 1.1 copy.30
  (4 shorter events, 0.0 us)
Async XLA Ops:
  2.4 3.9 %copy-start.3 = (f32[8,768]{1,0:T(8,128)}, f32[8,768]{1,0:T(8,128)S(1)}, u32[]{:S(2)}) copy-start(f32[8,768]{1,0:T(8,128)S(1)} %dynamic_update_slice.3.gain_hbm) | copy-start | bytes 73732
  231.4 2.3 copy-start
  233.8 6.3 %copy-start.2 = (bf16[512,768]{1,0:T(8,128)(2,1)S(1)}, bf16[512,768]{1,0:T(8,128)(2,1)}, u32[]{:S(2)}) copy-start(bf16[512,768]{1,0:T(8,128)(2,1)} %get-tuple-element.74) | copy-start | bytes 2359300
  233.8 7.2 %copy-start.1 = (f32[512,768]{1,0:T(8,128)S(1)}, f32[512,768]{1,0:T(8,128)}, u32[]{:S(2)}) copy-start(f32[512,768]{1,0:T(8,128)} %get-tuple-element.75) | copy-start | bytes 4718596

commit v2 on v1

--- a/solution.py
+++ b/solution.py
@@ -102,6 +102,22 @@
     return jnp.where((lane < 64) == (which == 0), 1.0, 0.0).astype(BF16)
 
 
+def own_length(lengths, assignment, device):
+    total = jnp.int32(0)
+    for number in range(lengths.shape[0]):
+        total = total + jnp.where(assignment[number] == device, lengths[number], 0)
+    return total
+
+
+def rotation(start, length, tokens):
+    row = lax.broadcasted_iota(jnp.int32, (tokens, 128), 0)
+    lane = lax.broadcasted_iota(jnp.int32, (1, 128), 1)
+    half = HDIM // 2
+    frequency = jnp.exp((lane % half).astype(F32) * (-2.0 * math.log(ROPE_BASE) / HDIM))
+    angles = jnp.where(row < length, row + start, 0).astype(F32) * frequency
+    return jnp.cos(angles), jnp.sin(angles) * jnp.where(lane % HDIM < half, -1.0, 1.0)
+
+
 def norm_back(grad_normed, values, gain):
     scale = scale_of(values)
     scaled = gain * grad_normed
@@ -111,16 +127,20 @@
 
 
 def forward_kernel(
-    length, x_hbm, tables_hbm, gain_hbm, q_hbm, k_hbm, v_hbm, o_hbm, g_hbm, u_hbm, d_hbm,
+    lengths, assignment, positions, x_hbm, gain_hbm, q_hbm, k_hbm, v_hbm, o_hbm, g_hbm, u_hbm, d_hbm,
     w_out, qkv_out, nt_out, n2t_out, at_out, ht_out, hid_out, a_out, b_out, h1_out, lse_out, gain_out,
-    w, x, tables, gains, gain, normed, normed_t, qkv, bias, attended, lse, h1, ht, hid, a, b,
-    load, x_out, x_in, y_out, y_in, p_out, p_in, f_out, f_in, g_out, g_in, w_store, store, f_store,
+    tables_out,
+    w, x, tables, gains, gain, normed, normed_t, qkv, bias, attended, lse, lse_t, h1, ht, hid, a, b,
+    load, x_out, x_in, y_out, y_in, z_out, z_in, d_out, d_in, p_out, p_in, f_out, f_in, g_out, g_in,
+    w_store, store, f_store,
 ):
     shard, replica = lax.axis_index("shard"), lax.axis_index("replica")
     partner, across = toggle(shard, 1), toggle(shard, 2)
     opposite = toggle(across, 1)
-    beside = toggle(replica, 1)
-    side = replica % 2
+    beside, behind = toggle(replica, 1), toggle(replica, 2)
+    mine = replica % 4
+    quarter_beside, quarter_behind = toggle(mine, 1), toggle(mine, 2)
+    quarter_last = toggle(quarter_beside, 2)
     tokens, width = x.shape
 
     sources = [q_hbm, k_hbm, v_hbm, o_hbm]
@@ -134,15 +154,13 @@
     ]
     x_load = pltpu.make_async_copy(x_hbm, x, load.at[UNITS])
     gain_load = pltpu.make_async_copy(gain_hbm, gains.at[shard], load.at[UNITS + 1])
-    table_load = pltpu.make_async_copy(tables_hbm, tables, load.at[UNITS + 2])
     gain_load.start()
     for copy in loads:
         copy.start()
     x_load.start()
-    table_load.start()
 
     shard_peers = [at(partner, replica), at(across, replica), at(opposite, replica)]
-    greet(shard_peers + [at(shard, beside)])
+    greet(shard_peers + [at(shard, beside), at(shard, behind)])
 
     gain_load.wait()
     gain_copies = [
@@ -152,25 +170,39 @@
     for copy in gain_copies:
         copy.start()
 
-    half = ROWS // 2
+    quarter = ROWS // 4
 
     def part(unit, owner, which):
-        return w.at[unit, owner, span(which * half, half)]
+        return w.at[unit, owner, span(which * quarter, quarter)]
 
     def cross(unit):
-        piece = part(unit, shard, side)
+        piece = part(unit, shard, mine)
         return remote(piece, piece, x_out.at[unit], x_in.at[unit], at(across, replica))
 
     def share(unit):
         piece = w.at[unit, shard]
         return remote(piece, piece, p_out.at[unit], p_in.at[unit], at(partner, replica))
 
-    def hand(unit):
-        piece = part(unit, across, side)
+    def hand_beside(unit):
+        piece = part(unit, across, mine)
         return remote(piece, piece, y_out.at[unit], y_in.at[unit], at(shard, beside))
 
+    def hand_behind(unit):
+        piece = part(unit, across, mine)
+        return remote(piece, piece, z_out.at[unit], z_in.at[unit], at(shard, behind))
+
+    def hand_on(unit, odd):
+        piece = part(unit, across, quarter_beside if odd else quarter_behind)
+        peer = at(shard, behind if odd else beside)
+        return remote(piece, piece, d_out.at[unit], d_in.at[unit], peer)
+
+    def by_parity(unit, act):
+        for odd in range(2):
+            pl.when(unit % 2 == odd)(functools.partial(act, odd))
+
     def forward(unit, number):
-        piece = part(unit, across, side if number == 0 else 1 - side)
+        which = (mine, quarter_beside, quarter_behind, quarter_last)[number]
+        piece = part(unit, across, which)
         return remote(piece, piece, f_out.at[number, unit], f_in.at[number, unit], at(partner, replica))
 
     def keep(unit):
@@ -181,25 +213,34 @@
         cross(unit).start()
         share(unit).start()
 
+    def take_cross(unit):
+        cross(unit).wait_recv()
+        hand_beside(unit).start()
+        hand_behind(unit).start()
+        forward(unit, 0).start()
+
+    def take_hands(unit):
+        hand_behind(unit).wait_recv()
+        hand_beside(unit).wait_recv()
+        by_parity(unit, lambda odd: hand_on(unit, odd).start())
+        forward(unit, 1).start()
+        forward(unit, 2).start()
+
+    def take_last(unit):
+        by_parity(unit, lambda odd: hand_on(unit, odd).wait_recv())
+        forward(unit, 3).start()
+
+    def complete(unit):
+        share(unit).wait_recv()
+        for number in range(4):
+            forward(unit, number).wait_recv()
+        keep(unit).start()
+
+    stages = [(0, take_cross), (2, take_hands), (4, take_last), (5, complete)]
+
     def tick(time):
-        @pl.when(time < UNITS)
-        def _():
-            cross(time).wait_recv()
-            hand(time).start()
-            forward(time, 0).start()
-
-        @pl.when((time >= 1) & (time < UNITS + 1))
-        def _():
-            hand(time - 1).wait_recv()
-            forward(time - 1, 1).start()
-
-        @pl.when((time >= 2) & (time < UNITS + 2))
-        def _():
-            unit = time - 2
-            share(unit).wait_recv()
-            forward(unit, 0).wait_recv()
-            forward(unit, 1).wait_recv()
-            keep(unit).start()
+        for lag, stage in stages:
+            pl.when((time >= lag) & (time < UNITS + lag))(functools.partial(stage, time - lag))
 
     def ticks(first, last):
         def body(time, carry):
@@ -217,7 +258,9 @@
 
     row = lax.broadcasted_iota(jnp.int32, (tokens, tokens), 0)
     column = lax.broadcasted_iota(jnp.int32, (tokens, tokens), 1)
-    seen = (column <= row) & ((row < length[0]) | (column >= length[0]))
+    device = shard * lax.axis_size("replica") + replica
+    length = own_length(lengths, assignment, device)
+    seen = (column <= row) & ((row < length) | (column >= length))
     bias[...] = jnp.where(seen, 0.0, -jnp.inf)
 
     x_load.wait()
@@ -229,8 +272,9 @@
     normed[...] = (values * scale_of(values) * gain[0:1]).astype(BF16)
     normed_t[0] = normed[...].T
     save(normed_t.at[0], nt_out)
-    table_load.wait()
-    ticks(0, 5)
+    tables[0], tables[1] = rotation(positions[0], length, tokens)
+    save(tables, tables_out)
+    ticks(0, 8)
 
     def project(step, carry):
         which, tile = step // (tokens // TILE), step % (tokens // TILE)
@@ -246,6 +290,7 @@
 
     lax.fori_loop(0, 3 * (tokens // TILE), project, 0)
     save(qkv, qkv_out)
+    tick(8)
     lse[...] = jnp.zeros_like(lse)
 
     def attend(pair, carry):
@@ -271,13 +316,14 @@
             lse[rows] = logs
             first = lax.broadcasted_iota(jnp.int32, mixed[0].shape, 1) < 64
             attended[rows, columns] = jnp.where(first, mixed[0], mixed[1]).astype(BF16)
-        tick(5 + pair)
+        tick(9 + pair)
         return carry
 
     lax.fori_loop(0, HEADS // 2, attend, 0)
     normed_t[1] = attended[...].T
     save(normed_t.at[1], at_out)
-    save(lse, lse_out)
+    lse_t[...] = lse[...].T
+    save(lse_t, lse_out)
     for tile in range(tokens // TILE):
         rows = pl.ds(tile * TILE, TILE)
         hidden_one = x[rows].astype(F32) + dot(attended[rows], flat(w[3]))
@@ -317,18 +363,20 @@
             ht[piece, block] = turned[piece * ROWS : (piece + 1) * ROWS]
         for copy in f_copies(block):
             copy.start()
-        tick(11 + block)
+        tick(15 + block)
         return carry
 
     lax.fori_loop(0, FBLOCKS, feed, 0)
-    ticks(11 + FBLOCKS, UNITS + 2)
+    ticks(15 + FBLOCKS, UNITS + 5)
 
     def settle(unit, carry):
         cross(unit).wait_send()
         share(unit).wait_send()
-        hand(unit).wait_send()
-        forward(unit, 0).wait_send()
-        forward(unit, 1).wait_send()
+        hand_beside(unit).wait_send()
+        hand_behind(unit).wait_send()
+        by_parity(unit, lambda odd: hand_on(unit, odd).wait_send())
+        for number in range(4):
+            forward(unit, number).wait_send()
         keep(unit).wait()
         return carry
 
@@ -342,7 +390,7 @@
             copy.wait()
 
 
-def forward_pass(length, tokens, tables, gain_rows, weights):
+def forward_pass(scalars, tokens, gain_rows, weights):
     count, width = tokens.shape
     shape = jax.ShapeDtypeStruct
     outs = (
@@ -356,19 +404,20 @@
         shape((FBLOCKS, count, COLS), BF16),
         shape((FBLOCKS, count, COLS), BF16),
         shape((count, width), F32),
-        shape((count, 128), F32),
+        shape((128, count), F32),
         shape(gain_rows.shape, F32),
+        shape((2, count, 128), F32),
     )
     anywhere = pl.BlockSpec(memory_space=pl.ANY)
     return pl.pallas_call(
         forward_kernel,
         out_shape=outs,
-        in_specs=[pl.BlockSpec(memory_space=pltpu.SMEM)] + [anywhere] * 10,
+        in_specs=[pl.BlockSpec(memory_space=pltpu.SMEM)] * 3 + [anywhere] * 9,
         out_specs=[anywhere] * len(outs),
         scratch_shapes=[
             pltpu.VMEM((UNITS, SHARDS, ROWS, COLS), BF16),
             pltpu.VMEM((count, width), BF16),
-            pltpu.VMEM(tables.shape, F32),
+            pltpu.VMEM((2, count, 128), F32),
             pltpu.VMEM((SHARDS,) + gain_rows.shape, F32),
             pltpu.VMEM(gain_rows.shape, F32),
             pltpu.VMEM((count, width), BF16),
@@ -377,42 +426,48 @@
             pltpu.VMEM((count, count), F32),
             pltpu.VMEM((count, width), BF16),
             pltpu.VMEM((count, 128), F32),
+            pltpu.VMEM((128, count), F32),
             pltpu.VMEM((count, width), F32),
             pltpu.VMEM((FBLOCKS, FBLOCKS, ROWS, count), BF16),
             pltpu.VMEM((FBLOCKS, count, COLS), BF16),
             pltpu.VMEM((FBLOCKS, count, COLS), BF16),
             pltpu.VMEM((FBLOCKS, count, COLS), BF16),
-            DMA((UNITS + 3,)),
-            DMA((UNITS,)), DMA((UNITS,)), DMA((UNITS,)), DMA((UNITS,)), DMA((UNITS,)), DMA((UNITS,)),
-            DMA((2, UNITS)), DMA((2, UNITS)), DMA((3,)), DMA((3,)),
+            DMA((UNITS + 2,)),
+        ]
+        + [DMA((UNITS,))] * 10
+        + [
+            DMA((4, UNITS)), DMA((4, UNITS)), DMA((3,)), DMA((3,)),
             DMA((UNITS,)), DMA((8,)), DMA((FBLOCKS, 4)),
         ],
         compiler_params=pltpu.CompilerParams(
             collective_id=0, has_side_effects=True, vmem_limit_bytes=60 * 1024 * 1024
         ),
         name="forward_gather",
-    )(length, tokens, tables, gain_rows, *weights)
+    )(*scalars, tokens, gain_rows, *weights)
 
 
 def backward_kernel(
     factors, pack,
-    length, x_hbm, cot_hbm, tables_hbm, gain_hbm, w_hbm, qkv_hbm, nt_hbm, n2t_hbm, at_hbm, ht_hbm,
-    hid_hbm, a_hbm, b_hbm, h1_hbm, lse_hbm,
+    early, lengths, assignment, x_hbm, cot_hbm, w_hbm, qkv_hbm, nt_hbm, n2t_hbm, at_hbm, ht_hbm,
+    hid_hbm, a_hbm, b_hbm, h1_hbm, lse_hbm, gain_hbm, tables_hbm,
     sums_out, gain_out, output_out, grad_out,
     *refs,
 ):
     levels = len(factors)
     (grads, near, far, gain_sum, gain_got, x, gbt, gain, turned, h1, acc, result, out_low) = refs[:13]
     parts = refs[13 : 13 + levels]
-    sems = refs[13 + levels :]
-    load, s_load, near_out, near_in, far_out, far_in, store, gain_send, gain_recv = sems[:9]
+    both = refs[13 + levels]
+    sems = refs[14 + levels :]
+    (load, s_load, near_out, near_in, far_out, far_in, store, gain_send, gain_recv) = sems[:9]
+    both_out, both_in, ht_sem = sems[9:12]
     down_out, down_in, up_out, up_in = (
-        sems[9 + kind * levels : 9 + (kind + 1) * levels] for kind in range(4)
+        sems[12 + kind * levels : 12 + (kind + 1) * levels] for kind in range(4)
     )
     shard, replica = lax.axis_index("shard"), lax.axis_index("replica")
     partner, across = toggle(shard, 1), toggle(shard, 2)
     opposite = toggle(across, 1)
     tokens, width = x.shape
+    length = own_length(lengths, assignment, shard * lax.axis_size("replica") + replica)
     groups = [ring(replica, members, stride) for members, stride in factors]
     flips = [at(partner, replica), at(across, replica)]
     stride, replicas = 1, math.prod(members for members, _ in factors)
@@ -476,6 +531,49 @@
             grads.at[unit, across], far.at[unit], far_out.at[unit], far_in.at[unit], at(across, replica)
         )
 
+    def is_early(unit):
+        return (unit >= early[0]) & (unit < early[1])
+
+    def when_early(unit, act, otherwise):
+        if early[0] == early[1]:
+            otherwise()
+            return
+        pl.when(is_early(unit))(act)
+        pl.when((unit < early[0]) | (unit >= early[1]))(otherwise)
+
+    def kept_half(ref, unit):
+        rows = ROWS // 2
+        return ref.at[unit, span(my_places[0] * rows, rows)]
+
+    def both_copy(unit, which):
+        rows = ROWS // 2
+        theirs = span((1 - my_places[0]) * rows, rows)
+        return remote(
+            grads.at[unit, across if which == 0 else shard, theirs],
+            both.at[unit - early[0], which],
+            both_out.at[unit - early[0], which],
+            both_in.at[unit - early[0], which],
+            at(shard, groups[0][1][0]),
+        )
+
+    def far_half(unit):
+        rows = ROWS // 2
+        return remote(
+            grads.at[unit, across, span(my_places[0] * rows, rows)],
+            kept_half(far, unit),
+            far_out.at[unit],
+            far_in.at[unit],
+            at(across, replica),
+        )
+
+    def take_both(unit):
+        rows = span(my_places[0] * (ROWS // 2), ROWS // 2)
+        both_copy(unit, 0).wait_recv()
+        grads[unit, across, rows] = plus(grads[unit, across, rows], both[unit - early[0], 0])
+        far_half(unit).start()
+        both_copy(unit, 1).wait_recv()
+        grads[unit, shard, rows] = plus(grads[unit, shard, rows], both[unit - early[0], 1])
+
     def down_copy(level, chunk, step):
         members = factors[level][0]
         place, others = groups[level]
@@ -519,18 +617,33 @@
     def take_near(unit):
         near_copy(unit, 0).wait_recv()
         grads[unit, across] = plus(grads[unit, across], near[unit, 0])
-        far_copy(unit).start()
+        when_early(unit, lambda: both_copy(unit, 0).start(), lambda: far_copy(unit).start())
         near_copy(unit, 1).wait_recv()
         grads[unit, shard] = plus(grads[unit, shard], near[unit, 1])
+        when_early(unit, lambda: both_copy(unit, 1).start(), lambda: None)
 
     def take_far(chunk):
         for piece in range(pack):
             unit = chunk * pack + piece
             near_copy(unit, 0).wait_send()
             near_copy(unit, 1).wait_send()
-            far_copy(unit).wait_recv()
-            grads[unit, shard] = plus(grads[unit, shard], far[unit])
-        over(0, lambda step: down_copy(0, chunk, step).start())
+
+            def whole():
+                far_copy(unit).wait_recv()
+                grads[unit, shard] = plus(grads[unit, shard], far[unit])
+
+            def half():
+                rows = span(my_places[0] * (ROWS // 2), ROWS // 2)
+                far_half(unit).wait_recv()
+                grads[unit, shard, rows] = plus(grads[unit, shard, rows], kept_half(far, unit)[...])
+
+            when_early(unit, half, whole)
+
+        when_early(
+            chunk,
+            lambda: over(1, lambda step: down_copy(1, chunk, step).start()),
+            lambda: over(0, lambda step: down_copy(0, chunk, step).start()),
+        )
 
     def take_down(level, chunk):
         over(level, lambda step: down_copy(level, chunk, step).wait_recv())
@@ -552,8 +665,11 @@
         else:
             store_copy(chunk).start()
 
-    stages = [take_far]
-    stages += [functools.partial(take_down, level) for level in range(levels)]
+    def take_first(chunk):
+        when_early(chunk, lambda: None, lambda: take_down(0, chunk))
+
+    stages = [take_far, take_first]
+    stages += [functools.partial(take_down, level) for level in range(1, levels)]
     stages += [functools.partial(take_up, level) for level in reversed(range(levels))]
     last_post = pack * (chunks + len(stages) - 1)
 
@@ -576,9 +692,9 @@
         )
 
     row = lax.broadcasted_iota(jnp.int32, (tokens, 1), 0)
-    valid = jnp.where(row < length[0], 1.0, 0.0)
-
-    def feed_forward(ht, down_w, gate_w, up_w, hid, a, b, grad_pair):
+    valid = jnp.where(row < length, 1.0, 0.0)
+
+    def feed_forward(ht, down_w, gate_w, up_w, hid, grad_pair):
         def stream(block):
             slot = block % 2
             pairs = [
@@ -586,27 +702,33 @@
                 (w_hbm.at[4 + 2 * block], gate_w.at[slot]),
                 (w_hbm.at[5 + 2 * block], up_w.at[slot]),
                 (hid_hbm.at[block], hid.at[slot]),
-                (a_hbm.at[block], a.at[slot]),
-                (b_hbm.at[block], b.at[slot]),
+                (a_hbm.at[block], grad_pair.at[slot, 0]),
+                (b_hbm.at[block], grad_pair.at[slot, 1]),
             ]
             return [
                 pltpu.make_async_copy(source, target, s_load.at[slot, number])
                 for number, (source, target) in enumerate(pairs)
             ]
 
-        ht_load = fetch(ht_hbm, ht, 7)
+        ht_loads = [
+            pltpu.make_async_copy(ht_hbm.at[unit], ht.at[unit], ht_sem.at[unit])
+            for unit in range(FBLOCKS)
+        ]
+        for copy in ht_loads:
+            copy.start()
         for copy in stream(0):
             copy.start()
         cot_load.wait()
         gbt[...] = (gbt[...].astype(F32) * valid).astype(BF16)
-        ht_load.wait()
 
         def down_grads(unit, carry):
+            pltpu.make_async_copy(ht_hbm.at[unit], ht.at[unit], ht_sem.at[unit]).wait()
             for owner in range(SHARDS // 2):
                 pair = pl.ds(2 * owner, 2)
                 product = dot(flat(ht[unit, pair]), gbt[...]).astype(BF16)
                 grads[unit, pair] = product.reshape(2, ROWS, COLS)
             give(unit)
+            pl.when(unit >= 1)(lambda: take_near(unit - 1))
             return carry
 
         lax.fori_loop(0, FBLOCKS, down_grads, 0)
@@ -628,19 +750,23 @@
             def rows_of(tile, inner):
                 rows = span(tile * TILE, TILE)
                 grad_hidden = dot_nt(gbt[rows], flat(down_w[slot]))
-                grad_pair[0, rows] = (grad_hidden * a[slot, rows].astype(F32)).astype(BF16)
-                grad_pair[1, rows] = (grad_hidden * b[slot, rows].astype(F32)).astype(BF16)
+                grad_pair[slot, 0, rows] = (
+                    grad_hidden * grad_pair[slot, 0, rows].astype(F32)
+                ).astype(BF16)
+                grad_pair[slot, 1, rows] = (
+                    grad_hidden * grad_pair[slot, 1, rows].astype(F32)
+                ).astype(BF16)
                 return inner
 
             lax.fori_loop(0, tokens // TILE, rows_of, 0)
-            pl.when(block == 0)(lambda: take_near(0))
+            pl.when(block == 0)(lambda: take_near(FBLOCKS - 1))
 
             def kind_of(kind, inner):
                 unit = FBLOCKS + 2 * block + kind
                 for owner in range(SHARDS // 2):
                     pair = pl.ds(2 * owner, 2)
                     product = dot(
-                        turned[0, pl.ds(2 * owner * ROWS, 2 * ROWS)], grad_pair[kind]
+                        turned[0, pl.ds(2 * owner * ROWS, 2 * ROWS)], grad_pair[slot, kind]
                     ).astype(BF16)
                     grads[unit, pair] = product.reshape(2, ROWS, COLS)
                 give(unit)
@@ -650,13 +776,13 @@
 
             @pl.when(block == 0)
             def _():
-                for unit in range(1, FBLOCKS):
-                    take_near(unit)
+                for unit in range(*early):
+                    take_both(unit)
 
             def back_rows(tile, inner):
                 rows = span(tile * TILE, TILE)
-                acc[rows] += dot_nt(grad_pair[0, rows], flat(gate_w[slot])) + dot_nt(
-                    grad_pair[1, rows], flat(up_w[slot])
+                acc[rows] += dot_nt(grad_pair[slot, 0, rows], flat(gate_w[slot])) + dot_nt(
+                    grad_pair[slot, 1, rows], flat(up_w[slot])
                 )
                 result[rows] += dot(hid[slot, rows], flat(down_w[slot]))
                 return inner
@@ -676,15 +802,13 @@
         pltpu.VMEM((2, SHARDS, ROWS, COLS), BF16),
         pltpu.VMEM((2, SHARDS, ROWS, COLS), BF16),
         pltpu.VMEM((2, tokens, COLS), BF16),
-        pltpu.VMEM((2, tokens, COLS), BF16),
-        pltpu.VMEM((2, tokens, COLS), BF16),
-        pltpu.VMEM((2, tokens, COLS), BF16),
+        pltpu.VMEM((2, 2, tokens, COLS), BF16),
     )
 
     def attention(attn_w, tables, qkv, lse, bias, grad_attended, grad_qkv):
         w_load = fetch(w_hbm.at[pl.ds(0, 4)], attn_w, 8)
         qkv_load = fetch(qkv_hbm, qkv, 9)
-        lse_load = fetch(lse_hbm, lse, 10)
+        lse_load = fetch(lse_hbm.at[pl.ds(0, 16)], lse, 10)
         table_load = fetch(tables_hbm, tables, 11)
         h1_load.wait()
         gain_load.wait()
@@ -693,7 +817,7 @@
         for tile in range(tokens // TILE):
             rows = pl.ds(tile * TILE, TILE)
             good = jnp.where(
-                lax.broadcasted_iota(jnp.int32, (TILE, 1), 0) + tile * TILE < length[0], 1.0, 0.0
+                lax.broadcasted_iota(jnp.int32, (TILE, 1), 0) + tile * TILE < length, 1.0, 0.0
             )
             out_low[rows] = ((h1[rows] + result[rows]) * good).astype(BF16)
             gain_piece, back = norm_back(acc[rows], h1[rows], gain[1:2])
@@ -720,7 +844,7 @@
 
         key_row = lax.broadcasted_iota(jnp.int32, (tokens, tokens), 0)
         query_column = lax.broadcasted_iota(jnp.int32, (tokens, tokens), 1)
-        seen = (key_row <= query_column) & ((query_column < length[0]) | (key_row >= length[0]))
+        seen = (key_row <= query_column) & ((query_column < length) | (key_row >= length))
         bias[...] = jnp.where(seen, 0.0, -jnp.inf)
         qkv_load.wait()
         lse_load.wait()
@@ -740,7 +864,7 @@
                     mask = head_mask(which)
                     query_one = query * mask
                     mixed_one = grad_mixed * mask
-                    log_row = lse[2 * pair + which, :, rows]
+                    log_row = lse[pl.ds(2 * pair + which, 1), rows]
                     probs, grad_probs = [], []
                     row_dot = jnp.zeros((1, TILE), F32)
                     for block in range(tile + 1):
@@ -811,7 +935,7 @@
         pltpu.VMEM((4, SHARDS, ROWS, COLS), BF16),
         pltpu.VMEM((2, tokens, 128), F32),
         pltpu.VMEM((3, tokens, width), BF16),
-        pltpu.VMEM((HEADS, 1, tokens), F32),
+        pltpu.VMEM((16, tokens), F32),
         pltpu.VMEM((tokens, tokens), F32),
         pltpu.VMEM((tokens, width), BF16),
         pltpu.VMEM((3, tokens, width), BF16),
@@ -839,9 +963,21 @@
 
     def settle(chunk, carry):
         for piece in range(pack):
-            far_copy(chunk * pack + piece).wait_send()
+            unit = chunk * pack + piece
+            when_early(
+                unit, lambda: far_half(unit).wait_send(), lambda: far_copy(unit).wait_send()
+            )
+
+        def both_sends():
+            both_copy(chunk, 0).wait_send()
+            both_copy(chunk, 1).wait_send()
+
+        when_early(
+            chunk, both_sends, lambda: over(0, lambda step: down_copy(0, chunk, step).wait_send())
+        )
         for level in range(levels):
-            over(level, lambda step: down_copy(level, chunk, step).wait_send())
+            if level > 0:
+                over(level, lambda step: down_copy(level, chunk, step).wait_send())
             over(level, lambda step: up_copy(level, chunk, step).wait_send())
         store_copy(chunk).wait()
         return carry
@@ -851,13 +987,16 @@
         gain_copy(step).wait_send()
 
 
-def backward_pass(length, tokens, cotangent, tables, gain, saved):
+def backward_pass(scalars, tokens, cotangent, saved):
     count, width = tokens.shape
     replicas = lax.axis_size("replica")
     factors, pack = replica_factors(replicas)
     levels = len(factors)
     chunks = UNITS // pack
     flips = 2 + replicas.bit_length() - 1
+    early = (0, 0) if pack == 1 else (0, 0)
+    spare = max(early[1] - early[0], 1)
+    gain = saved[-2]
     part_shapes = []
     units, rows, columns = pack, ROWS, COLS
     for level, (members, _) in enumerate(factors):
@@ -871,14 +1010,14 @@
     anywhere = pl.BlockSpec(memory_space=pl.ANY)
     shape = jax.ShapeDtypeStruct
     return pl.pallas_call(
-        functools.partial(backward_kernel, factors, pack),
+        functools.partial(backward_kernel, factors, pack, early),
         out_shape=(
             shape((UNITS, ROWS, COLS), BF16),
             shape(gain.shape, F32),
             shape((count, width), BF16),
             shape((count, width), F32),
         ),
-        in_specs=[pl.BlockSpec(memory_space=pltpu.SMEM)] + [anywhere] * (4 + len(saved)),
+        in_specs=[pl.BlockSpec(memory_space=pltpu.SMEM)] * 2 + [anywhere] * (2 + len(saved)),
         out_specs=[anywhere, pl.BlockSpec(memory_space=pltpu.VMEM), anywhere, anywhere],
         scratch_shapes=[
             pltpu.VMEM((UNITS, SHARDS, ROWS, COLS), BF16),
@@ -897,34 +1036,55 @@
         ]
         + [pltpu.VMEM(part, BF16) for part in part_shapes]
         + [
+            pltpu.VMEM((spare, 2, ROWS // 2, COLS), BF16),
+
             DMA((14,)), DMA((2, 6)), DMA((UNITS, 2)), DMA((UNITS, 2)), DMA((UNITS,)), DMA((UNITS,)),
-            DMA((chunks,)), DMA((flips,)), DMA((flips,)),
+            DMA((chunks,)), DMA((flips,)), DMA((flips,)), DMA((spare, 2)), DMA((spare, 2)), DMA((FBLOCKS,)),
         ]
         + [DMA(count_) for _ in range(4) for count_ in counts],
         compiler_params=pltpu.CompilerParams(
             collective_id=1, has_side_effects=True, vmem_limit_bytes=67043328
         ),
         name="backward_reduce",
-    )(length, tokens, cotangent, tables, gain, *saved)
-
-
-def widen_kernel(units, *refs):
-    outs, (low, wide, in_sem, out_sem) = refs[:7], refs[7:]
-    down, gate, up, out, query, key, value = outs
+    )(*scalars, tokens, cotangent, *saved)
+
+
+def finish_kernel(
+    sums, gain_sums, output_in, grad_in,
+    down, gate, up, out, query, key, value, gain_one, gain_two, output, grad,
+    low, wide, held_output, held_grad, in_sem, out_sem,
+):
     targets = [down.at[pl.ds(piece * ROWS, ROWS)] for piece in range(FBLOCKS)]
     for block in range(FBLOCKS):
         columns = pl.ds(block * COLS, COLS)
         targets += [gate.at[:, columns], up.at[:, columns]]
     targets += [out, query, key, value]
+    moves = [(output_in, held_output, output), (grad_in, held_grad, grad)]
     ins = [
-        pltpu.make_async_copy(units.at[unit], low.at[unit], in_sem.at[unit]) for unit in range(UNITS)
+        pltpu.make_async_copy(sums.at[unit], low.at[unit], in_sem.at[unit]) for unit in range(UNITS)
+    ]
+    ins += [
+        pltpu.make_async_copy(source, held, in_sem.at[UNITS + number])
+        for number, (source, held, _) in enumerate(moves)
     ]
     puts = [
         pltpu.make_async_copy(wide.at[unit], target, out_sem.at[unit])
         for unit, target in enumerate(targets)
     ]
-    for copy in ins:
+    puts += [
+        pltpu.make_async_copy(held, target, out_sem.at[UNITS + number])
+        for number, (_, held, target) in enumerate(moves)
+    ]
+    for copy in ins[UNITS:] + ins[:UNITS]:
         copy.start()
+    share = gain_sums.shape[1] // SHARDS
+    shard = lax.axis_index("shard")
+    turned = pltpu.roll(gain_sums[...], (SHARDS - shard) % SHARDS * share, 1)
+    gain_one[...] = turned[0:1, :share]
+    gain_two[...] = turned[1:2, :share]
+    for number in range(UNITS, UNITS + len(moves)):
+        ins[number].wait()
+        puts[number].start()
     for unit in range(UNITS):
         ins[unit].wait()
         wide[unit] = low[unit].astype(F32)
@@ -933,60 +1093,72 @@
         copy.wait()
 
 
-def widen(units):
+def finish(sums, gain_sums, output, input_grad):
     shape = jax.ShapeDtypeStruct
     small, broad = shape((ROWS, COLS), F32), shape((ROWS, FBLOCKS * COLS), F32)
-    anywhere = pl.BlockSpec(memory_space=pl.ANY)
+    share = shape((1, gain_sums.shape[1] // SHARDS), F32)
+    hbm, vmem = pl.BlockSpec(memory_space=pltpu.HBM), pl.BlockSpec(memory_space=pltpu.VMEM)
     return pl.pallas_call(
-        widen_kernel,
-        out_shape=(shape((FBLOCKS * ROWS, COLS), F32), broad, broad, small, small, small, small),
-        in_specs=[anywhere],
-        out_specs=[anywhere] * 7,
+        finish_kernel,
+        out_shape=(
+            shape((FBLOCKS * ROWS, COLS), F32), broad, broad, small, small, small, small, share, share,
+            shape(output.shape, output.dtype), shape(input_grad.shape, F32),
+        ),
+        in_specs=[hbm, vmem, hbm, hbm],
+        out_specs=[hbm] * 7 + [vmem] * 2 + [hbm] * 2,
         scratch_shapes=[
             pltpu.VMEM((UNITS, ROWS, COLS), BF16),
             pltpu.VMEM((UNITS, ROWS, COLS), F32),
-            DMA((UNITS,)),
-            DMA((UNITS,)),
+            pltpu.VMEM(output.shape, output.dtype),
+            pltpu.VMEM(input_grad.shape, F32),
+            DMA((UNITS + 2,)),
+            DMA((UNITS + 2,)),
         ],
-        compiler_params=pltpu.CompilerParams(vmem_limit_bytes=24 * 1024 * 1024),
-        name="widen",
-    )(units)
+        compiler_params=pltpu.CompilerParams(vmem_limit_bytes=67043328),
+        name="finish",
+    )(sums, gain_sums, output, input_grad)
 
 
 def per_device(
     tokens, cotangent, lengths, assignment, positions, attention_gain, query_weight, key_weight,
     value_weight, out_weight, feedforward_gain, gate_weight, up_weight, down_weight,
 ):
-    width = tokens.shape[1]
+    shard = lax.axis_index("shard")
+    lane = lax.broadcasted_iota(jnp.int32, (8, tokens.shape[1]), 1)
+    row = lax.broadcasted_iota(jnp.int32, (8, tokens.shape[1]), 0)
     share = attention_gain.shape[0]
-    shard = lax.axis_index("shard")
-    device = shard * lax.axis_size("replica") + lax.axis_index("replica")
-    length = jnp.sum(jnp.where(assignment == device, lengths, 0)).reshape(1)
-
-    half = HDIM // 2
-    lane = jnp.arange(128)
-    frequency = jnp.exp((lane % half).astype(F32) * (-2.0 * math.log(ROPE_BASE) / HDIM))
-    angles = positions.astype(F32)[:, None] * frequency[None, :]
-    sign = jnp.where(lane % HDIM < half, -1.0, 1.0)
-    tables = jnp.stack([jnp.cos(angles), jnp.sin(angles) * sign[None, :]])
-
-    gain_rows = jnp.stack([attention_gain, feedforward_gain]).astype(F32)
-    gain_rows = lax.dynamic_update_slice(jnp.zeros((8, width), F32), gain_rows, (0, shard * share))
-
-    w, qkv, nt, n2t, att, ht, hid, a, b, h1, lse, gain = forward_pass(
-        length,
+    spread = [
+        jnp.broadcast_to(gain, (SHARDS, share)).reshape(1, -1).astype(F32)
+        for gain in (attention_gain, feedforward_gain)
+    ]
+    gain_rows = jnp.where(
+        (lane // share == shard) & (row < 2), jnp.where(row == 0, spread[0], spread[1]), 0.0
+    )
+    saved = forward_pass(
+        [lengths, assignment, positions],
         tokens,
-        tables,
         gain_rows,
         [query_weight, key_weight, value_weight, out_weight, gate_weight, up_weight, down_weight],
     )
-    lse = lse[:, :HEADS].T.reshape(HEADS, 1, -1)
     sums, gain_sums, output, input_grad = backward_pass(
-        length, tokens, cotangent, tables, gain, [w, qkv, nt, n2t, att, ht, hid, a, b, h1, lse]
+        [lengths, assignment], tokens, cotangent, saved
     )
-    down, gate, up, out, query, key, value = widen(sums)
-    mine = lax.dynamic_slice(gain_sums, (0, shard * share), (2, share))
-    return output, input_grad, mine[0], query, key, value, out, mine[1], gate, up, down
+    down, gate, up, out, query, key, value, gain_one, gain_two, output, input_grad = finish(
+        sums, gain_sums, output, input_grad
+    )
+    return (
+        output,
+        input_grad,
+        gain_one.reshape(-1),
+        query,
+        key,
+        value,
+        out,
+        gain_two.reshape(-1),
+        gate,
+        up,
+        down,
+    )
 
 
 def solution(mesh):

time: 242 us -> 216 us (0.89)
  Pallas kernels: 228 us -> 213 us
  local copies, waits for them, and re-layouts: 9.23 us -> 1.48 us
  other arithmetic: 3.83 us -> 0.7 us
    pallas_call x1, Pallas kernels: 74.8 us -> 59.9 us  [forward_pass(): pl.pallas_call(forward_kernel, out_shape=outs, in_specs=[pl.BlockSpec(mem...]
    unnamed x10 -> x0, local copies, waits for them, and re-layouts: 4.37 us -> none
where the time goes in v2:
time: 216 us
  Pallas kernels  213 us (99%)
    pallas_call x1, Pallas kernels, backward_pass(): pl.pallas_call(functools.partial(backward_kernel, factors, pack, early),...  145 us
    pallas_call x1, Pallas kernels, forward_pass(): pl.pallas_call(forward_kernel, out_shape=outs, in_specs=[pl.BlockSpec(mem...  59.9 us
    pallas_call x1, Pallas kernels, finish(): pl.pallas_call(finish_kernel, out_shape=(shape((FBLOCKS * ROWS, COLS), F3...  7.6 us

profile of v2, /device:TPU:0, one launch (start us, length us, event | category | flops | bytes accessed | tf_op | source)
XLA Modules:
  0.0 215.6 jit_solution(15608717507111854435)
XLA Ops:
  0.7 0.7 broadcast_in_dim.26
  1.3 0.1 convert_element_type.25
  1.4 0.7 broadcast_in_dim.28
  2.1 0.1 convert_element_type.27
  2.2 0.7 select_select_fusion.gain_hbm
  2.8 59.9 %forward_gather.1 = (bf16[16,4,192,768]{3,2,1,0:T(8,128)(2,1)}, bf16[3,512,768]{2,1,0:T(8,128)(2,1)}, bf16[768,512]{1,0:T(8,128)(2,1)}, bf16[768,512]{1,0:T(8,12...) custom-call(s32[32]{0:T(128)} %lengths.3, ...), custom_call_target="tpu_custom_call" | custom-call | tf_op jit(solution)/shard_map/forward_gather/pallas_call | solution.py:412
  62.7 145.1 %backward_reduce.1 = (bf16[16,192,768]{2,1,0:T(8,128)(2,1)}, f32[8,768]{1,0:T(8,128)}, bf16[512,768]{1,0:T(8,128)(2,1)}, f32[512,768]{1,0:T(8,128)}) custom-call(s32[32]{0:T(128)} %lengths.3, s32[32]{0:T(128)} %assignment.3, bf16[512,768]{1,0:T(8,128)(2,1)} %x_hbm.3, bf16[512,768]{1,0:T(8,128)(2,1)} %cot_hbm.1, ...), custom_call_target="tpu_custom_call" | custom-call | tf_op jit(solution)/shard_map/backward_reduce/pallas_call | solution.py:1012
  207.9 7.6 %finish.1 = (f32[768,768]{1,0:T(8,128)}, f32[192,3072]{1,0:T(8,128)}, f32[192,3072]{1,0:T(8,128)}, f32[192,768]{1,0:T(8,128)}, f32[192,768]{1,0:T(8,128)}, /*ind...) custom-call(bf16[16,192,768]{2,1,0:T(8,128)(2,1)} %get-tuple-element, ...), custom_call_target="tpu_custom_call" | custom-call | tf_op jit(solution)/shard_map/finish/pallas_call | solution.py:1101
  (3 shorter events, 0.0 us)

commit v3 on v2

--- a/solution.py
+++ b/solution.py
@@ -23,6 +23,7 @@
 FBLOCKS = 4
 SHARDS = 4
 TILE = 256
+TALL = 512
 
 
 def toggle(index, stride):
@@ -65,11 +66,68 @@
     return pl.ds(mult(start, step), size)
 
 
-def replica_factors(count):
-    if count == 8:
-        return [(2, 1), (4, 2)], 1
-    assert count == 32
-    return [(2, 16), (4, 4), (4, 1)], 4
+class Levels:
+    def __init__(self, replica, count):
+        self.replica = replica
+        if count == 8:
+            self.pack, self.members, self.strides = 1, [2, 4], [1, 2]
+            self.cuts = [("rows", 2), ("quarters", 4)]
+        else:
+            assert count == 32
+            self.pack, self.members, self.strides = 4, [2, 4, 4], [16, 4, 1]
+            self.cuts = [("units", 2), ("halves", 4), ("quarters", 4)]
+        self.count = len(self.members)
+        self.whole = UNITS // self.pack
+        self.items = [(chunk, None) for chunk in range(self.whole)]
+        self.items += [
+            (chunk, third) for chunk in range(self.whole, UNITS // self.pack) for third in range(3)
+        ]
+
+    def item(self, chunk, third):
+        return chunk if third is None else self.whole + 3 * (chunk - self.whole) + third
+
+    def group(self, level, chunk):
+        return ring(self.replica, self.members[level], self.strides[level])
+
+    def places(self, chunk):
+        return [self.group(level, chunk)[0] for level in range(self.count)]
+
+    def size(self, level):
+        units, rows, columns = self.pack, ROWS, COLS
+        for kind, _ in self.cuts[:level]:
+            if kind == "units":
+                units = units // 2
+            elif kind == "rows":
+                rows = rows // 2
+            elif kind == "columns":
+                columns = columns // 2
+            elif kind == "halves":
+                units, rows = units // 2, rows // 2
+            else:
+                rows, columns = rows // 2, columns // 2
+        return units, rows, columns
+
+    def region(self, chunk, third, places):
+        unit, row, column = chunk * self.pack, 0, 0
+        parts = 1
+        if third is not None:
+            parts, column = 3, third * (COLS // 3)
+        for level, place in enumerate(places):
+            kind = self.cuts[level][0]
+            units, rows, columns = self.size(level + 1)
+            columns = columns // parts
+            if kind == "units":
+                unit = unit + place * units
+            elif kind == "rows":
+                row = row + place * rows
+            elif kind == "columns":
+                column = column + place * columns
+            elif kind == "halves":
+                unit, row = unit + place // 2 * units, row + place % 2 * rows
+            else:
+                row, column = row + place // 2 * rows, column + place % 2 * columns
+        units, rows, columns = self.size(len(places))
+        return pl.ds(unit, units), span(row, rows), span(column, columns // parts, 128)
 
 
 def dot(a, b):
@@ -447,30 +505,29 @@
 
 
 def backward_kernel(
-    factors, pack,
-    early, lengths, assignment, x_hbm, cot_hbm, w_hbm, qkv_hbm, nt_hbm, n2t_hbm, at_hbm, ht_hbm,
+    replicas,
+    lengths, assignment, x_hbm, cot_hbm, w_hbm, qkv_hbm, nt_hbm, n2t_hbm, at_hbm, ht_hbm,
     hid_hbm, a_hbm, b_hbm, h1_hbm, lse_hbm, gain_hbm, tables_hbm,
     sums_out, gain_out, output_out, grad_out,
     *refs,
 ):
-    levels = len(factors)
-    (grads, near, far, gain_sum, gain_got, x, gbt, gain, turned, h1, acc, result, out_low) = refs[:13]
-    parts = refs[13 : 13 + levels]
-    both = refs[13 + levels]
-    sems = refs[14 + levels :]
+    shard, replica = lax.axis_index("shard"), lax.axis_index("replica")
+    order = Levels(replica, replicas)
+    levels, pack = order.count, order.pack
+    (grads, near, far, gain_sum, gain_got, gbt, gain, n2t, h1, acc, result) = refs[:11]
+    parts = refs[11 : 11 + levels]
+    sems = refs[11 + levels :]
     (load, s_load, near_out, near_in, far_out, far_in, store, gain_send, gain_recv) = sems[:9]
-    both_out, both_in, ht_sem = sems[9:12]
+    ht_sem = sems[9]
     down_out, down_in, up_out, up_in = (
-        sems[12 + kind * levels : 12 + (kind + 1) * levels] for kind in range(4)
+        sems[10 + kind * levels : 10 + (kind + 1) * levels] for kind in range(4)
     )
-    shard, replica = lax.axis_index("shard"), lax.axis_index("replica")
     partner, across = toggle(shard, 1), toggle(shard, 2)
     opposite = toggle(across, 1)
-    tokens, width = x.shape
+    tokens, width = gbt.shape
     length = own_length(lengths, assignment, shard * lax.axis_size("replica") + replica)
-    groups = [ring(replica, members, stride) for members, stride in factors]
     flips = [at(partner, replica), at(across, replica)]
-    stride, replicas = 1, math.prod(members for members, _ in factors)
+    stride = 1
     while stride < replicas:
         flips.append(at(shard, toggle(replica, stride)))
         stride *= 2
@@ -481,40 +538,19 @@
         return copy
 
     cot_load = fetch(cot_hbm, gbt, 0)
-    n2t_load = fetch(n2t_hbm, turned.at[0], 1)
+    n2t_load = fetch(n2t_hbm, n2t, 1)
     h1_load = fetch(h1_hbm, h1, 2)
-    x_load = fetch(x_hbm, x, 3)
     gain_load = fetch(gain_hbm, gain, 4)
-    at_load = fetch(at_hbm, turned.at[1], 5)
-    nt_load = fetch(nt_hbm, turned.at[2], 6)
 
     greet(
         [at(partner, replica), at(across, replica)]
-        + [at(shard, other) for _, others in groups for other in others]
+        + [at(shard, other) for level in range(levels) for other in order.group(level, 0)[1]]
     )
 
     chunks = UNITS // pack
 
-    def region(chunk, places):
-        unit, units, row, rows, column, columns = chunk * pack, pack, 0, ROWS, 0, COLS
-        for level, place in enumerate(places):
-            if level == levels - 1:
-                rows, columns = rows // 2, columns // 2
-                row = row + (place // 2) * rows
-                column = column + (place % 2) * columns
-                continue
-            members = factors[level][0]
-            by_unit = math.gcd(units, members)
-            by_row = members // by_unit
-            units, rows = units // by_unit, rows // by_row
-            unit = unit + (place // by_row) * units
-            row = row + (place % by_row) * rows
-        return pl.ds(unit, units), span(row, rows), span(column, columns, 128)
-
-    my_places = [place for place, _ in groups]
-
-    def view(owner, chunk, places):
-        units, rows, columns = region(chunk, places)
+    def view(owner, chunk, third, places):
+        units, rows, columns = order.region(chunk, third, places)
         return grads.at[units, owner, rows, columns]
 
     def near_copy(unit, which):
@@ -526,82 +562,59 @@
             at(partner, replica),
         )
 
-    def far_copy(unit):
+    def columns_of(third, width):
+        return pl.ds(0, width) if third is None else pl.ds(third * (width // 3), width // 3)
+
+    def far_copy(unit, third=None):
+        columns = columns_of(third, COLS)
+        item = order.item(unit, third)
         return remote(
-            grads.at[unit, across], far.at[unit], far_out.at[unit], far_in.at[unit], at(across, replica)
-        )
-
-    def is_early(unit):
-        return (unit >= early[0]) & (unit < early[1])
-
-    def when_early(unit, act, otherwise):
-        if early[0] == early[1]:
-            otherwise()
-            return
-        pl.when(is_early(unit))(act)
-        pl.when((unit < early[0]) | (unit >= early[1]))(otherwise)
-
-    def kept_half(ref, unit):
-        rows = ROWS // 2
-        return ref.at[unit, span(my_places[0] * rows, rows)]
-
-    def both_copy(unit, which):
-        rows = ROWS // 2
-        theirs = span((1 - my_places[0]) * rows, rows)
-        return remote(
-            grads.at[unit, across if which == 0 else shard, theirs],
-            both.at[unit - early[0], which],
-            both_out.at[unit - early[0], which],
-            both_in.at[unit - early[0], which],
-            at(shard, groups[0][1][0]),
-        )
-
-    def far_half(unit):
-        rows = ROWS // 2
-        return remote(
-            grads.at[unit, across, span(my_places[0] * rows, rows)],
-            kept_half(far, unit),
-            far_out.at[unit],
-            far_in.at[unit],
+            grads.at[unit, across, :, columns],
+            far.at[unit, :, columns],
+            far_out.at[item],
+            far_in.at[item],
             at(across, replica),
         )
 
-    def take_both(unit):
-        rows = span(my_places[0] * (ROWS // 2), ROWS // 2)
-        both_copy(unit, 0).wait_recv()
-        grads[unit, across, rows] = plus(grads[unit, across, rows], both[unit - early[0], 0])
-        far_half(unit).start()
-        both_copy(unit, 1).wait_recv()
-        grads[unit, shard, rows] = plus(grads[unit, shard, rows], both[unit - early[0], 1])
-
-    def down_copy(level, chunk, step):
-        members = factors[level][0]
-        place, others = groups[level]
+    def part(level, chunk, third, step):
+        width = order.size(level + 1)[2]
+        return parts[level].at[chunk, step, :, :, columns_of(third, width)]
+
+    def down_copy(level, chunk, step, third=None):
+        members = order.members[level]
+        place, others = order.group(level, chunk)
         theirs = (place + step + 1) % members
+        item = order.item(chunk, third)
         return remote(
-            view(shard, chunk, my_places[:level] + [theirs]),
-            parts[level].at[chunk, step],
-            down_out[level].at[chunk, step],
-            down_in[level].at[chunk, step],
+            view(shard, chunk, third, order.places(chunk)[:level] + [theirs]),
+            part(level, chunk, third, step),
+            down_out[level].at[item, step],
+            down_in[level].at[item, step],
             at(shard, others[step]),
         )
 
-    def up_copy(level, chunk, step):
-        piece = view(partner, chunk, my_places[: level + 1])
+    def up_copy(level, chunk, step, third=None):
+        piece = view(partner, chunk, third, order.places(chunk)[: level + 1])
+        item = order.item(chunk, third)
         return remote(
             piece,
             piece,
-            up_out[level].at[chunk, step],
-            up_in[level].at[chunk, step],
-            at(shard, groups[level][1][step]),
+            up_out[level].at[item, step],
+            up_in[level].at[item, step],
+            at(shard, order.group(level, chunk)[1][step]),
         )
 
-    def store_copy(chunk):
+    def store_copy(chunk, third=None):
         units = pl.ds(chunk * pack, pack)
-        return pltpu.make_async_copy(grads.at[units, partner], sums_out.at[units], store.at[chunk])
+        columns = columns_of(third, COLS)
+        return pltpu.make_async_copy(
+            grads.at[units, partner, :, columns],
+            sums_out.at[units, :, columns],
+            store.at[order.item(chunk, third)],
+        )
 
     def over(level, act):
-        for step in range(factors[level][0] - 1):
+        for step in range(order.members[level] - 1):
             act(step)
 
     def give(unit):
@@ -617,61 +630,55 @@
     def take_near(unit):
         near_copy(unit, 0).wait_recv()
         grads[unit, across] = plus(grads[unit, across], near[unit, 0])
-        when_early(unit, lambda: both_copy(unit, 0).start(), lambda: far_copy(unit).start())
+        if pack > 1:
+            far_copy(unit).start()
+        else:
+            pl.when(unit < order.whole)(lambda: far_copy(unit).start())
+
+            @pl.when(unit >= order.whole)
+            def _():
+                for third in range(3):
+                    far_copy(unit, third).start()
+
         near_copy(unit, 1).wait_recv()
         grads[unit, shard] = plus(grads[unit, shard], near[unit, 1])
-        when_early(unit, lambda: both_copy(unit, 1).start(), lambda: None)
-
-    def take_far(chunk):
+
+    def take_far(chunk, third=None):
         for piece in range(pack):
             unit = chunk * pack + piece
-            near_copy(unit, 0).wait_send()
-            near_copy(unit, 1).wait_send()
-
-            def whole():
-                far_copy(unit).wait_recv()
-                grads[unit, shard] = plus(grads[unit, shard], far[unit])
-
-            def half():
-                rows = span(my_places[0] * (ROWS // 2), ROWS // 2)
-                far_half(unit).wait_recv()
-                grads[unit, shard, rows] = plus(grads[unit, shard, rows], kept_half(far, unit)[...])
-
-            when_early(unit, half, whole)
-
-        when_early(
-            chunk,
-            lambda: over(1, lambda step: down_copy(1, chunk, step).start()),
-            lambda: over(0, lambda step: down_copy(0, chunk, step).start()),
-        )
-
-    def take_down(level, chunk):
-        over(level, lambda step: down_copy(level, chunk, step).wait_recv())
-        places = my_places[: level + 1]
-        terms = [view(shard, chunk, places)[...]]
-        terms += [parts[level][chunk, step] for step in range(factors[level][0] - 1)]
+            if third is None or third == 0:
+                near_copy(unit, 0).wait_send()
+                near_copy(unit, 1).wait_send()
+            far_copy(unit, third).wait_recv()
+            columns = columns_of(third, COLS)
+            grads[unit, shard, :, columns] = plus(
+                grads[unit, shard, :, columns], far[unit, :, columns]
+            )
+        over(0, lambda step: down_copy(0, chunk, step, third).start())
+
+    def take_down(level, chunk, third=None):
+        over(level, lambda step: down_copy(level, chunk, step, third).wait_recv())
+        places = order.places(chunk)[: level + 1]
+        terms = [view(shard, chunk, third, places)[...]]
+        terms += [part(level, chunk, third, step)[...] for step in range(order.members[level] - 1)]
         total = plus(*terms)
         if level + 1 < levels:
-            view(shard, chunk, places)[...] = total
-            over(level + 1, lambda step: down_copy(level + 1, chunk, step).start())
+            view(shard, chunk, third, places)[...] = total
+            over(level + 1, lambda step: down_copy(level + 1, chunk, step, third).start())
         else:
-            view(partner, chunk, places)[...] = total
-            over(level, lambda step: up_copy(level, chunk, step).start())
-
-    def take_up(level, chunk):
-        over(level, lambda step: up_copy(level, chunk, step).wait_recv())
+            view(partner, chunk, third, places)[...] = total
+            over(level, lambda step: up_copy(level, chunk, step, third).start())
+
+    def take_up(level, chunk, third=None):
+        over(level, lambda step: up_copy(level, chunk, step, third).wait_recv())
         if level > 0:
-            over(level - 1, lambda step: up_copy(level - 1, chunk, step).start())
+            over(level - 1, lambda step: up_copy(level - 1, chunk, step, third).start())
         else:
-            store_copy(chunk).start()
-
-    def take_first(chunk):
-        when_early(chunk, lambda: None, lambda: take_down(0, chunk))
-
-    stages = [take_far, take_first]
-    stages += [functools.partial(take_down, level) for level in range(1, levels)]
+            store_copy(chunk, third).start()
+
+    stages = [take_far]
+    stages += [functools.partial(take_down, level) for level in range(levels)]
     stages += [functools.partial(take_up, level) for level in reversed(range(levels))]
-    last_post = pack * (chunks + len(stages) - 1)
 
     def post(time):
         step = (time + 1) // pack - 1
@@ -679,12 +686,16 @@
             good = (step >= lag) & (step < chunks + lag) & ((time + 1) % pack == 0)
             pl.when(good)(functools.partial(stage, step - lag))
 
-    def posts(first, last):
-        def body(time, carry):
-            post(time)
-            return carry
-
-        lax.fori_loop(first, last, body, 0)
+    def remaining(first):
+        arrival, found = 0.0, []
+        for chunk, third in order.items:
+            pace = 1.0 if third is None else 1.0 / 3
+            arrival += pace
+            wait = (0.0, 1.02, 2.02, 3.02, 4.02) if third is None else (0.0, 0.68, 1.36, 2.04, 2.72)
+            for lag, stage in enumerate(stages):
+                if chunk + lag >= first:
+                    found.append((arrival + wait[lag], lag, len(found), stage, chunk, third))
+        return [entry[3:] for entry in sorted(found, key=lambda entry: entry[:3])]
 
     def gain_copy(step):
         return remote(
@@ -694,7 +705,27 @@
     row = lax.broadcasted_iota(jnp.int32, (tokens, 1), 0)
     valid = jnp.where(row < length, 1.0, 0.0)
 
-    def feed_forward(ht, down_w, gate_w, up_w, hid, grad_pair):
+    def down_phase(ht):
+        ht_loads = [
+            pltpu.make_async_copy(ht_hbm.at[unit], ht.at[unit], ht_sem.at[unit])
+            for unit in range(FBLOCKS)
+        ]
+        for copy in ht_loads:
+            copy.start()
+        cot_load.wait()
+        gbt[...] = (gbt[...].astype(F32) * valid).astype(BF16)
+
+        def down_grads(unit, carry):
+            pltpu.make_async_copy(ht_hbm.at[unit], ht.at[unit], ht_sem.at[unit]).wait()
+            product = dot(flat(ht[unit]), gbt[...]).astype(BF16)
+            grads[unit] = product.reshape(SHARDS, ROWS, COLS)
+            give(unit)
+            pl.when(unit >= 1)(lambda: take_near(unit - 1))
+            return carry
+
+        lax.fori_loop(0, FBLOCKS, down_grads, 0)
+
+    def feed_forward(down_w, gate_w, up_w, hid, grad_pair):
         def stream(block):
             slot = block % 2
             pairs = [
@@ -710,28 +741,8 @@
                 for number, (source, target) in enumerate(pairs)
             ]
 
-        ht_loads = [
-            pltpu.make_async_copy(ht_hbm.at[unit], ht.at[unit], ht_sem.at[unit])
-            for unit in range(FBLOCKS)
-        ]
-        for copy in ht_loads:
-            copy.start()
         for copy in stream(0):
             copy.start()
-        cot_load.wait()
-        gbt[...] = (gbt[...].astype(F32) * valid).astype(BF16)
-
-        def down_grads(unit, carry):
-            pltpu.make_async_copy(ht_hbm.at[unit], ht.at[unit], ht_sem.at[unit]).wait()
-            for owner in range(SHARDS // 2):
-                pair = pl.ds(2 * owner, 2)
-                product = dot(flat(ht[unit, pair]), gbt[...]).astype(BF16)
-                grads[unit, pair] = product.reshape(2, ROWS, COLS)
-            give(unit)
-            pl.when(unit >= 1)(lambda: take_near(unit - 1))
-            return carry
-
-        lax.fori_loop(0, FBLOCKS, down_grads, 0)
         n2t_load.wait()
         acc[...] = jnp.zeros_like(acc)
         result[...] = jnp.zeros_like(result)
@@ -747,57 +758,35 @@
             for copy in stream(block):
                 copy.wait()
 
-            def rows_of(tile, inner):
-                rows = span(tile * TILE, TILE)
-                grad_hidden = dot_nt(gbt[rows], flat(down_w[slot]))
-                grad_pair[slot, 0, rows] = (
-                    grad_hidden * grad_pair[slot, 0, rows].astype(F32)
-                ).astype(BF16)
-                grad_pair[slot, 1, rows] = (
-                    grad_hidden * grad_pair[slot, 1, rows].astype(F32)
-                ).astype(BF16)
-                return inner
-
-            lax.fori_loop(0, tokens // TILE, rows_of, 0)
+            grad_hidden = dot_nt(gbt[...], flat(down_w[slot]))
+            grad_pair[slot, 0] = (grad_hidden * grad_pair[slot, 0].astype(F32)).astype(BF16)
+            grad_pair[slot, 1] = (grad_hidden * grad_pair[slot, 1].astype(F32)).astype(BF16)
             pl.when(block == 0)(lambda: take_near(FBLOCKS - 1))
 
             def kind_of(kind, inner):
                 unit = FBLOCKS + 2 * block + kind
-                for owner in range(SHARDS // 2):
-                    pair = pl.ds(2 * owner, 2)
-                    product = dot(
-                        turned[0, pl.ds(2 * owner * ROWS, 2 * ROWS)], grad_pair[slot, kind]
-                    ).astype(BF16)
-                    grads[unit, pair] = product.reshape(2, ROWS, COLS)
+                product = dot(n2t[...], grad_pair[slot, kind]).astype(BF16)
+                grads[unit] = product.reshape(SHARDS, ROWS, COLS)
                 give(unit)
                 return inner
 
             lax.fori_loop(0, 2, kind_of, 0)
 
-            @pl.when(block == 0)
-            def _():
-                for unit in range(*early):
-                    take_both(unit)
-
-            def back_rows(tile, inner):
-                rows = span(tile * TILE, TILE)
-                acc[rows] += dot_nt(grad_pair[slot, 0, rows], flat(gate_w[slot])) + dot_nt(
-                    grad_pair[slot, 1, rows], flat(up_w[slot])
-                )
-                result[rows] += dot(hid[slot, rows], flat(down_w[slot]))
-                return inner
-
-            lax.fori_loop(0, tokens // TILE, back_rows, 0)
+            post(2 * block - block // 3)
+            acc[...] += dot_nt(grad_pair[slot, 0], flat(gate_w[slot])) + dot_nt(
+                grad_pair[slot, 1], flat(up_w[slot])
+            )
+            result[...] += dot(hid[slot], flat(down_w[slot]))
             take_near(FBLOCKS + 2 * block)
             take_near(FBLOCKS + 2 * block + 1)
-            post(block)
+            pl.when(block != 2)(lambda: post(2 * block + 1 - block // 3))
             return carry
 
         lax.fori_loop(0, FBLOCKS, block_step, 0)
 
+    pl.run_scoped(down_phase, pltpu.VMEM((FBLOCKS, FBLOCKS, ROWS, tokens), BF16))
     pl.run_scoped(
         feed_forward,
-        pltpu.VMEM((FBLOCKS, FBLOCKS, ROWS, tokens), BF16),
         pltpu.VMEM((2, FBLOCKS, ROWS, COLS), BF16),
         pltpu.VMEM((2, SHARDS, ROWS, COLS), BF16),
         pltpu.VMEM((2, SHARDS, ROWS, COLS), BF16),
@@ -805,11 +794,14 @@
         pltpu.VMEM((2, 2, tokens, COLS), BF16),
     )
 
-    def attention(attn_w, tables, qkv, lse, bias, grad_attended, grad_qkv):
+    def attention(attn_w, tables, qkv, lse, bias, grad_attended, grad_qkv, turned, x, out_low):
+        at_load = fetch(at_hbm, turned.at[0], 5)
         w_load = fetch(w_hbm.at[pl.ds(0, 4)], attn_w, 8)
         qkv_load = fetch(qkv_hbm, qkv, 9)
         lse_load = fetch(lse_hbm.at[pl.ds(0, 16)], lse, 10)
         table_load = fetch(tables_hbm, tables, 11)
+        nt_load = fetch(nt_hbm, turned.at[1], 6)
+        x_load = fetch(x_hbm, x, 3)
         h1_load.wait()
         gain_load.wait()
 
@@ -830,22 +822,20 @@
         output_store = pltpu.make_async_copy(out_low, output_out, load.at[12])
         output_store.start()
         at_load.wait()
-        for owner in range(SHARDS // 2):
-            pair = pl.ds(2 * owner, 2)
-            product = dot(turned[1, pl.ds(2 * owner * ROWS, 2 * ROWS)], gbt[...]).astype(BF16)
-            grads[UNITS - 4, pair] = product.reshape(2, ROWS, COLS)
+        product = dot(turned[0], gbt[...]).astype(BF16)
+        grads[UNITS - 4] = product.reshape(SHARDS, ROWS, COLS)
         give(UNITS - 4)
         w_load.wait()
         for tile in range(tokens // TILE):
             rows = pl.ds(tile * TILE, TILE)
             grad_attended[rows] = dot_nt(gbt[rows], flat(attn_w[3])).astype(BF16)
         take_near(UNITS - 4)
-        post(FBLOCKS)
+        post(7)
 
         key_row = lax.broadcasted_iota(jnp.int32, (tokens, tokens), 0)
         query_column = lax.broadcasted_iota(jnp.int32, (tokens, tokens), 1)
         seen = (key_row <= query_column) & ((query_column < length) | (key_row >= length))
-        bias[...] = jnp.where(seen, 0.0, -jnp.inf)
+        bias[...] = jnp.where(seen, 0.0, -jnp.inf).astype(BF16)
         qkv_load.wait()
         lse_load.wait()
         table_load.wait()
@@ -870,7 +860,7 @@
                     for block in range(tile + 1):
                         keys = pl.ds(block * TILE, TILE)
                         scores = dot_nt(qkv[1, keys, columns], query_one) * inv_root
-                        prob = jnp.exp(scores + bias[keys, rows] - log_row)
+                        prob = jnp.exp(scores + bias[keys, rows].astype(F32) - log_row)
                         grad_value[block] += dot(prob.astype(BF16), mixed_one)
                         grad_prob = dot_nt(qkv[2, keys, columns], mixed_one)
                         row_dot = row_dot + jnp.sum(prob * grad_prob, axis=0, keepdims=True)
@@ -890,19 +880,15 @@
                 back = back * tables[0, keys] - half_swap(back) * tables[1, keys]
                 grad_qkv[1, keys, columns] = back.astype(BF16)
                 grad_qkv[2, keys, columns] = grad_value[block].astype(BF16)
-            post(FBLOCKS + 1 + pair)
+            pl.when(pair % 2 == 1)(lambda: post(8 + pair // 2))
             return carry
 
         lax.fori_loop(0, HEADS // 2, attend_back, 0)
         nt_load.wait()
 
         def projection(which, carry):
-            for owner in range(SHARDS // 2):
-                pair = pl.ds(2 * owner, 2)
-                product = dot(
-                    turned[2, pl.ds(2 * owner * ROWS, 2 * ROWS)], grad_qkv[which]
-                ).astype(BF16)
-                grads[UNITS - 3 + which, pair] = product.reshape(2, ROWS, COLS)
+            product = dot(turned[1], grad_qkv[which]).astype(BF16)
+            grads[UNITS - 3 + which] = product.reshape(SHARDS, ROWS, COLS)
             give(UNITS - 3 + which)
             return carry
 
@@ -910,9 +896,7 @@
         acc[...] = jnp.zeros_like(acc)
 
         def input_back(which, carry):
-            for tile in range(tokens // TILE):
-                rows = pl.ds(tile * TILE, TILE)
-                acc[rows] += dot_nt(grad_qkv[which, rows], flat(attn_w[which]))
+            acc[...] += dot_nt(grad_qkv[which], flat(attn_w[which]))
             take_near(UNITS - 3 + which)
             return carry
 
@@ -936,53 +920,47 @@
         pltpu.VMEM((2, tokens, 128), F32),
         pltpu.VMEM((3, tokens, width), BF16),
         pltpu.VMEM((16, tokens), F32),
-        pltpu.VMEM((tokens, tokens), F32),
+        pltpu.VMEM((tokens, tokens), BF16),
         pltpu.VMEM((tokens, width), BF16),
         pltpu.VMEM((3, tokens, width), BF16),
+        pltpu.VMEM((2, width, tokens), BF16),
+        pltpu.VMEM((tokens, width), BF16),
+        pltpu.VMEM((tokens, width), BF16),
     )
 
-    first = FBLOCKS + 1 + HEADS // 2
+    first = 11
     gain_copy(0).start()
 
-    def rest(time, carry):
-        post(time)
+    def gain_step(step):
+        gain_copy(step).wait_recv()
+        gain_sum[step + 1] = gain_sum[step] + gain_got[step]
+        if step + 1 < len(flips):
+            gain_copy(step + 1).start()
+
+    if pack > 1:
+        lax.fori_loop(first, pack * (chunks + len(stages) - 1), lambda time, _: (post(time), _)[1], 0)
         for step in range(len(flips)):
-
-            @pl.when(time == first + 1 + step)
-            def _():
-                gain_copy(step).wait_recv()
-                gain_sum[step + 1] = gain_sum[step] + gain_got[step]
-                if step + 1 < len(flips):
-                    gain_copy(step + 1).start()
-
-        return carry
-
-    assert first + 1 + len(flips) <= last_post
-    lax.fori_loop(first, last_post, rest, 0)
+            gain_step(step)
+    else:
+        plan = remaining(first)
+        for number, (stage, chunk, third) in enumerate(plan):
+            stage(chunk, third)
+            left = len(plan) - 1 - number
+            if left % 3 == 1 and left // 3 < len(flips):
+                gain_step(len(flips) - 1 - left // 3)
     gain_out[...] = gain_sum[len(flips)]
 
-    def settle(chunk, carry):
+    def settle(chunk, third=None):
         for piece in range(pack):
-            unit = chunk * pack + piece
-            when_early(
-                unit, lambda: far_half(unit).wait_send(), lambda: far_copy(unit).wait_send()
-            )
-
-        def both_sends():
-            both_copy(chunk, 0).wait_send()
-            both_copy(chunk, 1).wait_send()
-
-        when_early(
-            chunk, both_sends, lambda: over(0, lambda step: down_copy(0, chunk, step).wait_send())
-        )
+            far_copy(chunk * pack + piece, third).wait_send()
         for level in range(levels):
-            if level > 0:
-                over(level, lambda step: down_copy(level, chunk, step).wait_send())
-            over(level, lambda step: up_copy(level, chunk, step).wait_send())
-        store_copy(chunk).wait()
-        return carry
-
-    lax.fori_loop(0, chunks, settle, 0)
+            over(level, lambda step: down_copy(level, chunk, step, third).wait_send())
+            over(level, lambda step: up_copy(level, chunk, step, third).wait_send())
+        store_copy(chunk, third).wait()
+
+    lax.fori_loop(0, order.whole, lambda chunk, _: (settle(chunk), _)[1], 0)
+    for chunk, third in order.items[order.whole :]:
+        settle(chunk, third)
     for step in range(len(flips)):
         gain_copy(step).wait_send()
 
@@ -990,27 +968,19 @@
 def backward_pass(scalars, tokens, cotangent, saved):
     count, width = tokens.shape
     replicas = lax.axis_size("replica")
-    factors, pack = replica_factors(replicas)
-    levels = len(factors)
-    chunks = UNITS // pack
+    order = Levels(0, replicas)
+    chunks = UNITS // order.pack
     flips = 2 + replicas.bit_length() - 1
-    early = (0, 0) if pack == 1 else (0, 0)
-    spare = max(early[1] - early[0], 1)
     gain = saved[-2]
-    part_shapes = []
-    units, rows, columns = pack, ROWS, COLS
-    for level, (members, _) in enumerate(factors):
-        if level == levels - 1:
-            rows, columns = rows // 2, columns // 2
-        else:
-            by_unit = math.gcd(units, members)
-            units, rows = units // by_unit, rows // (members // by_unit)
-        part_shapes.append((chunks, members - 1, units, rows, columns))
-    counts = [(chunks, members - 1) for members, _ in factors]
+    part_shapes = [
+        (chunks, members - 1) + order.size(level + 1) for level, members in enumerate(order.members)
+    ]
+    items = max(len(order.items), UNITS)
+    counts = [(items, members - 1) for members in order.members]
     anywhere = pl.BlockSpec(memory_space=pl.ANY)
     shape = jax.ShapeDtypeStruct
     return pl.pallas_call(
-        functools.partial(backward_kernel, factors, pack, early),
+        functools.partial(backward_kernel, replicas),
         out_shape=(
             shape((UNITS, ROWS, COLS), BF16),
             shape(gain.shape, F32),
@@ -1026,20 +996,17 @@
             pltpu.VMEM((flips + 1,) + gain.shape, F32),
             pltpu.VMEM((flips,) + gain.shape, F32),
             pltpu.VMEM((count, width), BF16),
-            pltpu.VMEM((count, width), BF16),
             pltpu.VMEM(gain.shape, F32),
-            pltpu.VMEM((3, width, count), BF16),
+            pltpu.VMEM((width, count), BF16),
             pltpu.VMEM((count, width), F32),
             pltpu.VMEM((count, width), F32),
             pltpu.VMEM((count, width), F32),
-            pltpu.VMEM((count, width), BF16),
         ]
         + [pltpu.VMEM(part, BF16) for part in part_shapes]
         + [
-            pltpu.VMEM((spare, 2, ROWS // 2, COLS), BF16),
-
-            DMA((14,)), DMA((2, 6)), DMA((UNITS, 2)), DMA((UNITS, 2)), DMA((UNITS,)), DMA((UNITS,)),
-            DMA((chunks,)), DMA((flips,)), DMA((flips,)), DMA((spare, 2)), DMA((spare, 2)), DMA((FBLOCKS,)),
+
+            DMA((14,)), DMA((2, 6)), DMA((UNITS, 2)), DMA((UNITS, 2)), DMA((items,)), DMA((items,)),
+            DMA((items,)), DMA((flips,)), DMA((flips,)), DMA((FBLOCKS,)),
         ]
         + [DMA(count_) for _ in range(4) for count_ in counts],
         compiler_params=pltpu.CompilerParams(

time: 216 us -> 211 us (0.977)
  Pallas kernels: 213 us -> 208 us
    pallas_call x1, Pallas kernels: 145 us -> 140 us  [backward_pass(): pl.pallas_call(functools.partial(backward_kernel, replicas), out_shape=(s...]
where the time goes in v3:
time: 211 us
  Pallas kernels  208 us (99%)
    pallas_call x1, Pallas kernels, backward_pass(): pl.pallas_call(functools.partial(backward_kernel, replicas), out_shape=(s...  140 us
    pallas_call x1, Pallas kernels, forward_pass(): pl.pallas_call(forward_kernel, out_shape=outs, in_specs=[pl.BlockSpec(mem...  59.9 us
    pallas_call x1, Pallas kernels, finish(): pl.pallas_call(finish_kernel, out_shape=(shape((FBLOCKS * ROWS, COLS), F3...  7.6 us

profile of v3, /device:TPU:0, one launch (start us, length us, event | category | flops | bytes accessed | tf_op | source)
XLA Modules:
  0.0 210.8 jit_solution(5190528627408226138)
XLA Ops:
  0.7 0.7 broadcast_in_dim.26
  1.3 0.1 convert_element_type.25
  1.4 0.7 broadcast_in_dim.28
  2.1 0.1 convert_element_type.27
  2.2 0.7 select_select_fusion.gain_hbm
  2.8 59.9 %forward_gather.1 = (bf16[16,4,192,768]{3,2,1,0:T(8,128)(2,1)}, bf16[3,512,768]{2,1,0:T(8,128)(2,1)}, bf16[768,512]{1,0:T(8,128)(2,1)}, bf16[768,512]{1,0:T(8,12...) custom-call(s32[32]{0:T(128)} %lengths.3, ...), custom_call_target="tpu_custom_call" | custom-call | tf_op jit(solution)/shard_map/forward_gather/pallas_call | solution.py:470
  62.7 140.3 %backward_reduce.1 = (bf16[16,192,768]{2,1,0:T(8,128)(2,1)}, f32[8,768]{1,0:T(8,128)}, bf16[512,768]{1,0:T(8,128)(2,1)}, f32[512,768]{1,0:T(8,128)}) custom-call(s32[32]{0:T(128)} %lengths.3, s32[32]{0:T(128)} %assignment.3, bf16[512,768]{1,0:T(8,128)(2,1)} %x_hbm.3, bf16[512,768]{1,0:T(8,128)(2,1)} %cot_hbm.1, ...), custom_call_target="tpu_custom_call" | custom-call | tf_op jit(solution)/shard_map/backward_reduce/pallas_call | solution.py:982
  203.1 7.6 %finish.1 = (f32[768,768]{1,0:T(8,128)}, f32[192,3072]{1,0:T(8,128)}, f32[192,3072]{1,0:T(8,128)}, f32[192,768]{1,0:T(8,128)}, f32[192,768]{1,0:T(8,128)}, /*ind...) custom-call(bf16[16,192,768]{2,1,0:T(8,128)(2,1)} %get-tuple-element, ...), custom_call_target="tpu_custom_call" | custom-call | tf_op jit(solution)/shard_map/finish/pallas_call | solution.py:1068
  (3 shorter events, 0.0 us)

commit v4 on v3

--- a/solution.py
+++ b/solution.py
@@ -334,19 +334,17 @@
     save(tables, tables_out)
     ticks(0, 8)
 
-    def project(step, carry):
-        which, tile = step // (tokens // TILE), step % (tokens // TILE)
-        rows = span(tile * TILE, TILE)
-        product = dot(normed[rows], flat(w[which]))
-        cosine = jnp.where(which < 2, tables[0, rows], 1.0)
-        sine = jnp.where(which < 2, tables[1, rows], 0.0)
+    def project(which, carry):
+        product = dot(normed[...], flat(w[which]))
+        cosine = jnp.where(which < 2, tables[0], 1.0)
+        sine = jnp.where(which < 2, tables[1], 0.0)
         for pair in range(width // 128):
             columns = slice(pair * 128, pair * 128 + 128)
             piece = product[:, columns]
-            qkv[which, rows, columns] = (piece * cosine + half_swap(piece) * sine).astype(BF16)
+            qkv[which, :, columns] = (piece * cosine + half_swap(piece) * sine).astype(BF16)
         return carry
 
-    lax.fori_loop(0, 3 * (tokens // TILE), project, 0)
+    lax.fori_loop(0, 3, project, 0)
     save(qkv, qkv_out)
     tick(8)
     lse[...] = jnp.zeros_like(lse)
@@ -405,7 +403,7 @@
 
     def feed(block, carry):
         def rows_of(tile, inner):
-            rows = span(tile * TILE, TILE)
+            rows = span(tile * TALL, TALL)
             gate = dot(normed[rows], flat(w[4 + 2 * block]))
             upward = dot(normed[rows], flat(w[5 + 2 * block]))
             sigmoid = jax.nn.sigmoid(gate)
@@ -415,7 +413,7 @@
             b[block, rows] = activated.astype(BF16)
             return inner
 
-        lax.fori_loop(0, tokens // TILE, rows_of, 0)
+        lax.fori_loop(0, tokens // TALL, rows_of, 0)
         turned = hid[block].T
         for piece in range(FBLOCKS):
             ht[piece, block] = turned[piece * ROWS : (piece + 1) * ROWS]

time: 211 us -> 209 us (level)
  no operation moved by 1% of the time
where the time goes in v4:
time: 209 us
  Pallas kernels  206 us (99%)
    pallas_call x1, Pallas kernels, backward_pass(): pl.pallas_call(functools.partial(backward_kernel, replicas), out_shape=(s...  140 us
    pallas_call x1, Pallas kernels, forward_pass(): pl.pallas_call(forward_kernel, out_shape=outs, in_specs=[pl.BlockSpec(mem...  58.5 us
    pallas_call x1, Pallas kernels, finish(): pl.pallas_call(finish_kernel, out_shape=(shape((FBLOCKS * ROWS, COLS), F3...  7.6 us

profile of v4, /device:TPU:0, one launch (start us, length us, event | category | flops | bytes accessed | tf_op | source)
XLA Modules:
  0.0 209.2 jit_solution(9503329362262369067)
XLA Ops:
  0.7 0.7 broadcast_in_dim.26
  1.3 0.1 convert_element_type.25
  1.4 0.7 broadcast_in_dim.28
  2.1 0.1 convert_element_type.27
  2.2 0.7 select_select_fusion.gain_hbm
  2.8 58.5 %forward_gather.1 = (bf16[16,4,192,768]{3,2,1,0:T(8,128)(2,1)}, bf16[3,512,768]{2,1,0:T(8,128)(2,1)}, bf16[768,512]{1,0:T(8,128)(2,1)}, bf16[768,512]{1,0:T(8,12...) custom-call(s32[32]{0:T(128)} %lengths.3, ...), custom_call_target="tpu_custom_call" | custom-call | tf_op jit(solution)/shard_map/forward_gather/pallas_call | solution.py:468
  61.4 140.1 %backward_reduce.1 = (bf16[16,192,768]{2,1,0:T(8,128)(2,1)}, f32[8,768]{1,0:T(8,128)}, bf16[512,768]{1,0:T(8,128)(2,1)}, f32[512,768]{1,0:T(8,128)}) custom-call(s32[32]{0:T(128)} %lengths.3, s32[32]{0:T(128)} %assignment.3, bf16[512,768]{1,0:T(8,128)(2,1)} %x_hbm.3, bf16[512,768]{1,0:T(8,128)(2,1)} %cot_hbm.1, ...), custom_call_target="tpu_custom_call" | custom-call | tf_op jit(solution)/shard_map/backward_reduce/pallas_call | solution.py:980
  201.5 7.6 %finish.1 = (f32[768,768]{1,0:T(8,128)}, f32[192,3072]{1,0:T(8,128)}, f32[192,3072]{1,0:T(8,128)}, f32[192,768]{1,0:T(8,128)}, f32[192,768]{1,0:T(8,128)}, /*ind...) custom-call(bf16[16,192,768]{2,1,0:T(8,128)(2,1)} %get-tuple-element, ...), custom_call_target="tpu_custom_call" | custom-call | tf_op jit(solution)/shard_map/finish/pallas_call | solution.py:1066
  (3 shorter events, 0.0 us)

commit v5 on v4

--- a/solution.py
+++ b/solution.py
@@ -689,7 +689,7 @@
         for chunk, third in order.items:
             pace = 1.0 if third is None else 1.0 / 3
             arrival += pace
-            wait = (0.0, 1.02, 2.02, 3.02, 4.02) if third is None else (0.0, 0.68, 1.36, 2.04, 2.72)
+            wait = (0.0, 1.02, 2.02, 3.02, 5.02) if third is None else (0.0, 0.68, 1.36, 2.04, 2.72)
             for lag, stage in enumerate(stages):
                 if chunk + lag >= first:
                     found.append((arrival + wait[lag], lag, len(found), stage, chunk, third))
@@ -944,8 +944,8 @@
         for number, (stage, chunk, third) in enumerate(plan):
             stage(chunk, third)
             left = len(plan) - 1 - number
-            if left % 3 == 1 and left // 3 < len(flips):
-                gain_step(len(flips) - 1 - left // 3)
+            if left % 2 == 1 and left // 2 < len(flips):
+                gain_step(len(flips) - 1 - left // 2)
     gain_out[...] = gain_sum[len(flips)]
 
     def settle(chunk, third=None):

time: 209 us -> 209 us (level)
  no operation moved by 1% of the time
where the time goes in v5:
time: 209 us
  Pallas kernels  206 us (99%)
    pallas_call x1, Pallas kernels, backward_pass(): pl.pallas_call(functools.partial(backward_kernel, replicas), out_shape=(s...  140 us
    pallas_call x1, Pallas kernels, forward_pass(): pl.pallas_call(forward_kernel, out_shape=outs, in_specs=[pl.BlockSpec(mem...  58.5 us
    pallas_call x1, Pallas kernels, finish(): pl.pallas_call(finish_kernel, out_shape=(shape((FBLOCKS * ROWS, COLS), F3...  7.6 us

profile of v5, /device:TPU:0, one launch (start us, length us, event | category | flops | bytes accessed | tf_op | source)
XLA Modules:
  0.0 208.9 jit_solution(7355971444113272218)
XLA Ops:
  0.7 0.7 broadcast_in_dim.26
  1.3 0.1 convert_element_type.25
  1.4 0.7 broadcast_in_dim.28
  2.1 0.1 convert_element_type.27
  2.2 0.7 select_select_fusion.gain_hbm
  2.8 58.5 %forward_gather.1 = (bf16[16,4,192,768]{3,2,1,0:T(8,128)(2,1)}, bf16[3,512,768]{2,1,0:T(8,128)(2,1)}, bf16[768,512]{1,0:T(8,128)(2,1)}, bf16[768,512]{1,0:T(8,12...) custom-call(s32[32]{0:T(128)} %lengths.3, ...), custom_call_target="tpu_custom_call" | custom-call | tf_op jit(solution)/shard_map/forward_gather/pallas_call | solution.py:468
  61.4 139.7 %backward_reduce.1 = (bf16[16,192,768]{2,1,0:T(8,128)(2,1)}, f32[8,768]{1,0:T(8,128)}, bf16[512,768]{1,0:T(8,128)(2,1)}, f32[512,768]{1,0:T(8,128)}) custom-call(s32[32]{0:T(128)} %lengths.3, s32[32]{0:T(128)} %assignment.3, bf16[512,768]{1,0:T(8,128)(2,1)} %x_hbm.3, bf16[512,768]{1,0:T(8,128)(2,1)} %cot_hbm.1, ...), custom_call_target="tpu_custom_call" | custom-call | tf_op jit(solution)/shard_map/backward_reduce/pallas_call | solution.py:980
  201.1 7.6 %finish.1 = (f32[768,768]{1,0:T(8,128)}, f32[192,3072]{1,0:T(8,128)}, f32[192,3072]{1,0:T(8,128)}, f32[192,768]{1,0:T(8,128)}, f32[192,768]{1,0:T(8,128)}, /*ind...) custom-call(bf16[16,192,768]{2,1,0:T(8,128)(2,1)} %get-tuple-element, ...), custom_call_target="tpu_custom_call" | custom-call | tf_op jit(solution)/shard_map/finish/pallas_call | solution.py:1066
  (3 shorter events, 0.0 us)
